TPU v7x, 128 devices: a whole 4x4x4 slice. The times are simulated.
128 devices in a mesh: strip: 32 (over z, y_lo, x), wave: 4 (over y_hi, core).
Axes of the slice: x: 4, y: 4 (y_hi: 2, y_lo: 2; y = y_hi * 2 + y_lo), z: 4, core: 2. Of those that a mesh axis runs over, the one named last changes fastest.
Arguments:
- source: bfloat16 [64, 1024, 2, 512], P('strip', None, None, 'wave'), parts along dimension 3, may hold values from -4 to 4
- pivot_inverse_real: bfloat16 [64, 4096, 1024], P('strip', 'wave'), parts along dimension 1, may hold values from -1 to 1
- factor_imag: bfloat16 [64, 4096, 1024], P('strip', 'wave'), parts along dimension 1, may hold values from -1 to 1
Outputs:
- solution: bfloat16 [64, 1024, 2, 512], P('strip', None, None, 'wave'), parts along dimension 3
There are 4 independent parts, one for each index of `wave`. A program takes and returns all parts, laid end to end along the dimension named above; each array names one. Nothing has to cross between parts.
All inputs are finite; a program needn't handle non-finite values.
Results may differ from a plain program's by a relative error of at most 0.033.
Values may be sent and summed in bfloat16 or wider, within the bound.
No kernel may reach another device: no remote copies, remote signals or barrier semaphores. Data moves between devices by JAX's collectives and lax.ppermute only.
A program may use at most 64 MiB of HBM per device.

v0:
```python
import jax
import jax.numpy as jnp
from jax import lax
from jax.sharding import PartitionSpec as P

MICRO = 64


def shifted(value, axis, steps):
    count = lax.axis_size(axis)
    initial, last = (max(0, -steps), min(count, count - steps))
    return lax.ppermute(value, axis, [(source, source + steps) for source in range(initial, last)])


def complex_apply(real_part, imag_part, vector):
    mode_count, halves, columns = vector.shape
    merged = vector.reshape(mode_count, halves * columns)
    direct = jnp.dot(real_part, merged, preferred_element_type=jnp.float32).reshape(
        mode_count, halves, columns
    )
    crossed = jnp.dot(imag_part, merged, preferred_element_type=jnp.float32).reshape(
        mode_count, halves, columns
    )
    return jnp.stack([direct[:, 0] - crossed[:, 1], direct[:, 1] + crossed[:, 0]], axis=1)


def forward_block(block_source, pivot_inverse_real, factor_imag, incoming):
    traces = []
    trace_now = incoming
    for layer_index in range(block_source.shape[0]):
        summed = (block_source[layer_index].astype(jnp.float32) + trace_now).astype(jnp.bfloat16)
        trace_now = complex_apply(pivot_inverse_real[layer_index], factor_imag[layer_index], summed)
        traces.append(trace_now)
    return (jnp.stack(traces), trace_now)


def backward_block(block_traces, pivot_inverse_real, factor_imag, incoming):
    layer_count = block_traces.shape[0]
    fields = [None] * layer_count
    field_now = incoming
    for layer_index in reversed(range(layer_count)):
        field_now = block_traces[layer_index] + complex_apply(
            pivot_inverse_real[layer_index],
            factor_imag[layer_index],
            field_now.astype(jnp.bfloat16),
        )
        fields[layer_index] = field_now
    return (jnp.stack(fields), field_now.astype(jnp.bfloat16))


def shards(source, pivot_inverse_real, factor_imag):
    strips = lax.axis_size("strip")
    position = lax.axis_index("strip")
    layer_count, mode_count, halves, sources = source.shape
    block_size = MICRO // 2
    batches = sources // block_size
    empty = jnp.zeros((mode_count, halves, block_size), jnp.float32)
    empty_half = jnp.zeros((mode_count, halves, block_size), jnp.bfloat16)

    def advance(moment, state, back_start, do_forward, do_backward):
        down_send, up_send, traces, fields = state
        if do_forward:
            received = shifted(down_send, "strip", 1)
            which = moment - position
            active = jnp.logical_and(which >= 0, which < batches)
            offset = jnp.clip(which, 0, batches - 1) * block_size

            def compute_forward(current):
                block_source = lax.dynamic_slice_in_dim(source, offset, block_size, 3)
                new_traces, last_trace = forward_block(
                    block_source, pivot_inverse_real, factor_imag, received
                )
                return (lax.dynamic_update_slice_in_dim(current, new_traces, offset, 3), last_trace)

            def remain_forward(current):
                return (current, down_send)

            traces, down_send = lax.cond(active, compute_forward, remain_forward, traces)
        if do_backward:
            arrived = shifted(up_send, "strip", -1)
            which = moment - back_start - (strips - 1 - position)
            active = jnp.logical_and(which >= 0, which < batches)
            offset = jnp.clip(which, 0, batches - 1) * block_size

            def evaluate_backward_sweep(current):
                block_traces = lax.dynamic_slice_in_dim(traces, offset, block_size, 3)
                new_fields, first_field = backward_block(
                    block_traces, pivot_inverse_real, factor_imag, arrived
                )
                return (
                    lax.dynamic_update_slice_in_dim(
                        current, new_fields.astype(jnp.bfloat16), offset, 3
                    ),
                    first_field,
                )

            def remain_backward(current):
                return (current, up_send)

            fields, up_send = lax.cond(active, evaluate_backward_sweep, remain_backward, fields)
        return (down_send, up_send, traces, fields)

    state = (
        empty,
        empty_half,
        jnp.zeros(source.shape, jnp.float32),
        jnp.zeros(source.shape, jnp.bfloat16),
    )
    state = lax.fori_loop(
        0,
        strips + batches - 1,
        lambda moment, current: advance(moment, current, 0, True, False),
        state,
    )
    state = lax.fori_loop(
        0,
        strips + batches - 1,
        lambda moment, current: advance(moment, current, 0, False, True),
        state,
    )
    return state[3]


def solution(mesh):
    placed = (P("strip", None, None, "wave"), P("strip", "wave", None), P("strip", "wave", None))
    return jax.shard_map(
        shards,
        mesh=mesh,
        in_specs=placed,
        out_specs=P("strip", None, None, "wave"),
        check_vma=False,
    )
```

profile of v0, /device:TPU:8, one launch (start us, length us, event | category | flops | bytes accessed | tf_op | source)
XLA Modules:
  0.0 1218.8 jit_solution(17974605685914896630)
XLA Ops:
  3.4 520.0 %while.32 = (s32[]{:T(128)}, f32[1024,2,32]{0,2,1:T(8,128)}, f32[2,1024,2,128]{1,3,2,0:T(8,128)S(1)}, s32[]{:T(128)}, bf16[2,1024,2,128]{1,3,2,0:T(8,128)(2,1)S(...) while((s32[]{:T(128)}, f32[1024,2,32]{0,2,1:T(8,128)}, ...), condition=%wide.region_3.4_spmd, body=%wide.region_0.3_spmd.sunk | while | flops 537722880 | bytes 15991149 | solution.py:109
  6.8 8.8 collective-permute-done
  17.6 9.5 collective-permute-done
  29.0 8.6 collective-permute-done
  39.6 8.6 collective-permute-done
  50.2 35.5 %collective-permute-done = f32[1024,2,32]{0,2,1:T(8,128)S(1)} collective-permute-done((f32[1024,2,32]{0,2,1:T(8,128)}, f32[1024,2,32]{0,2,1:T(8,128)S(1)}, u32[]{:S(2)}, u32[]{:S(2)}) %collective-permute-start) | collective-permute-done | bytes 262176 | tf_op jit(solution)/shard_map/while/body/eval_jaxpr/ppermute | solution.py:12
  85.7 10.4 conditional.4
  98.0 8.6 collective-permute-done
  106.7 10.4 conditional.4
  119.0 8.6 collective-permute-done
  127.7 10.4 conditional.4
  140.0 8.6 collective-permute-done
  148.6 10.4 conditional.4
  161.0 10.4 collective-permute-done
  171.3 8.5 collective-permute-start
  189.2 7.7 collective-permute-done
  196.9 7.9 collective-permute-start
  213.4 9.2 collective-permute-done
  245.1 17.2 %collective-permute-start = (f32[1024,2,32]{0,2,1:T(8,128)}, f32[1024,2,32]{0,2,1:T(8,128)S(1)}, u32[]{:S(2)}, u32[]{:S(2)}) collective-permute-start(f32[1024,2,32]{0,2,1:T(8,128)} %get-tuple-element.561), channel_id=1, source_target_pairs={{0,4},{4,8},{8,12},{12,16},{16,20},{20,24},{24,28},{28,32},{32,36}... | collective-permute-start | bytes 786440 | tf_op jit(solution)/shard_map/while/body/eval_jaxpr/ppermute | solution.py:12
  266.5 8.9 collective-permute-start
  291.0 7.7 collective-permute-start
  314.6 12.7 %collective-permute-start = (f32[1024,2,32]{0,2,1:T(8,128)}, f32[1024,2,32]{0,2,1:T(8,128)S(1)}, u32[]{:S(2)}, u32[]{:S(2)}) collective-permute-start(f32[1024,2,32]{0,2,1:T(8,128)} %get-tuple-element.561), channel_id=1, source_target_pairs={{0,4},{4,8},{8,12},{12,16},{16,20},{20,24},{24,28},{28,32},{32,36}... | collective-permute-start | bytes 786440 | tf_op jit(solution)/shard_map/while/body/eval_jaxpr/ppermute | solution.py:12
  354.5 8.0 collective-permute-start
  378.2 9.4 collective-permute-start
  391.8 8.9 collective-permute-start
  404.9 8.8 collective-permute-start
  418.1 7.6 collective-permute-start
  431.2 15.0 %collective-permute-start = (f32[1024,2,32]{0,2,1:T(8,128)}, f32[1024,2,32]{0,2,1:T(8,128)S(1)}, u32[]{:S(2)}, u32[]{:S(2)}) collective-permute-start(f32[1024,2,32]{0,2,1:T(8,128)} %get-tuple-element.561), channel_id=1, source_target_pairs={{0,4},{4,8},{8,12},{12,16},{16,20},{20,24},{24,28},{28,32},{32,36}... | collective-permute-start | bytes 786440 | tf_op jit(solution)/shard_map/while/body/eval_jaxpr/ppermute | solution.py:12
  452.6 7.6 collective-permute-start
  465.5 8.5 collective-permute-start
  479.9 8.2 collective-permute-start
  492.2 15.5 %collective-permute-start = (f32[1024,2,32]{0,2,1:T(8,128)}, f32[1024,2,32]{0,2,1:T(8,128)S(1)}, u32[]{:S(2)}, u32[]{:S(2)}) collective-permute-start(f32[1024,2,32]{0,2,1:T(8,128)} %get-tuple-element.561), channel_id=1, source_target_pairs={{0,4},{4,8},{8,12},{12,16},{16,20},{20,24},{24,28},{28,32},{32,36}... | collective-permute-start | bytes 786440 | tf_op jit(solution)/shard_map/while/body/eval_jaxpr/ppermute | solution.py:12
  523.6 693.2 %while.33 = (s32[]{:T(128)}, bf16[1024,2,32]{0,2,1:T(8,128)(2,1)S(1)}, bf16[2,1024,2,128]{1,3,2,0:T(8,128)(2,1)S(1)}, s32[]{:T(128)}, f32[2,1024,2,128]{1,3,2,0:...) while((s32[]{:T(128)}, ...), condition=%wide.region_7.8_spmd, body=%wide.region_4.7_spmd.sunk | while | flops 538312704 | bytes 15204725 | solution.py:115
  525.5 11.1 collective-permute-done.1
  538.5 9.7 collective-permute-done.1
  560.0 7.7 collective-permute-done.1
  589.1 13.2 %collective-permute-done.1 = bf16[1024,2,32]{0,2,1:T(8,128)(2,1)S(1)} collective-permute-done((bf16[1024,2,32]{0,2,1:T(8,128)(2,1)S(1)}, bf16[1024,2,32]{0,2,1:T(8,128)(2,1)S(1)}, u32[]{:S(2)}, u32[]{:S(2)}) %collective-permute-start.1) | collective-permute-done | bytes 131104 | tf_op jit(solution)/shard_map/while/body/eval_jaxpr/ppermute | solution.py:12
  604.2 7.9 collective-permute-done.1
  614.1 12.6 %collective-permute-done.1 = bf16[1024,2,32]{0,2,1:T(8,128)(2,1)S(1)} collective-permute-done((bf16[1024,2,32]{0,2,1:T(8,128)(2,1)S(1)}, bf16[1024,2,32]{0,2,1:T(8,128)(2,1)S(1)}, u32[]{:S(2)}, u32[]{:S(2)}) %collective-permute-start.1) | collective-permute-done | bytes 131104 | tf_op jit(solution)/shard_map/while/body/eval_jaxpr/ppermute | solution.py:12
  628.6 10.8 collective-permute-done.1
  641.3 10.4 collective-permute-done.1
  653.7 10.1 collective-permute-done.1
  665.7 10.6 collective-permute-done.1
  687.6 14.2 %collective-permute-done.1 = bf16[1024,2,32]{0,2,1:T(8,128)(2,1)S(1)} collective-permute-done((bf16[1024,2,32]{0,2,1:T(8,128)(2,1)S(1)}, bf16[1024,2,32]{0,2,1:T(8,128)(2,1)S(1)}, u32[]{:S(2)}, u32[]{:S(2)}) %collective-permute-start.1) | collective-permute-done | bytes 131104 | tf_op jit(solution)/shard_map/while/body/eval_jaxpr/ppermute | solution.py:12
  703.7 7.9 collective-permute-done.1
  713.6 13.2 %collective-permute-done.1 = bf16[1024,2,32]{0,2,1:T(8,128)(2,1)S(1)} collective-permute-done((bf16[1024,2,32]{0,2,1:T(8,128)(2,1)S(1)}, bf16[1024,2,32]{0,2,1:T(8,128)(2,1)S(1)}, u32[]{:S(2)}, u32[]{:S(2)}) %collective-permute-start.1) | collective-permute-done | bytes 131104 | tf_op jit(solution)/shard_map/while/body/eval_jaxpr/ppermute | solution.py:12
  728.7 7.6 collective-permute-done.1
  738.9 9.2 collective-permute-done.1
  760.3 12.5 %collective-permute-done.1 = bf16[1024,2,32]{0,2,1:T(8,128)(2,1)S(1)} collective-permute-done((bf16[1024,2,32]{0,2,1:T(8,128)(2,1)S(1)}, bf16[1024,2,32]{0,2,1:T(8,128)(2,1)S(1)}, u32[]{:S(2)}, u32[]{:S(2)}) %collective-permute-start.1) | collective-permute-done | bytes 131104 | tf_op jit(solution)/shard_map/while/body/eval_jaxpr/ppermute | solution.py:12
  774.7 8.0 collective-permute-done.1
  784.6 7.7 collective-permute-done.1
  794.3 7.9 collective-permute-done.1
  804.1 8.1 collective-permute-done.1
  814.2 7.9 collective-permute-done.1
  824.0 10.1 collective-permute-done.1
  836.0 266.5 %collective-permute-done.1 = bf16[1024,2,32]{0,2,1:T(8,128)(2,1)S(1)} collective-permute-done((bf16[1024,2,32]{0,2,1:T(8,128)(2,1)S(1)}, bf16[1024,2,32]{0,2,1:T(8,128)(2,1)S(1)}, u32[]{:S(2)}, u32[]{:S(2)}) %collective-permute-start.1) | collective-permute-done | bytes 131104 | tf_op jit(solution)/shard_map/while/body/eval_jaxpr/ppermute | solution.py:12
  1102.5 9.7 conditional.5
  1114.1 10.3 collective-permute-done.1
  1124.4 9.7 conditional.5
  1136.1 7.6 collective-permute-done.1
  1143.7 9.7 conditional.5
  1163.0 9.7 conditional.5
  1179.6 13.7 %collective-permute-start.1 = (bf16[1024,2,32]{0,2,1:T(8,128)(2,1)S(1)}, bf16[1024,2,32]{0,2,1:T(8,128)(2,1)S(1)}, u32[]{:S(2)}, u32[]{:S(2)}) collective-permute-start(bf16[1024,2,32]{0,2,1:T(8,128)(2,1)S(1)} %get-tuple-element.591), channel_id=1, source_target_pairs={{4,0},{8,4},{12,8},{16,12},{20,16},{24,20},{28,24},{32,28},{36,32}... | collective-permute-start | bytes 393224 | tf_op jit(solution)/shard_map/while/body/eval_jaxpr/ppermute | solution.py:12
  1204.8 9.5 collective-permute-start.1
  (238 shorter events, 406.1 us)
Async XLA Ops:
  3.4 12.2 %collective-permute-start = (f32[1024,2,32]{0,2,1:T(8,128)}, f32[1024,2,32]{0,2,1:T(8,128)S(1)}, u32[]{:S(2)}, u32[]{:S(2)}) collective-permute-start(f32[1024,2,32]{0,2,1:T(8,128)} %get-tuple-element.561), channel_id=1, source_target_pairs={{0,4},{4,8},{8,12},{12,16},{16,20},{20,24},{24,28},{28,32},{32,36}... | collective-permute-start | bytes 786440 | tf_op jit(solution)/shard_map/while/body/eval_jaxpr/ppermute | solution.py:12
  15.7 11.4 collective-permute-start
  27.1 10.6 collective-permute-start
  37.7 10.6 collective-permute-start
  48.2 37.4 %collective-permute-start = (f32[1024,2,32]{0,2,1:T(8,128)}, f32[1024,2,32]{0,2,1:T(8,128)S(1)}, u32[]{:S(2)}, u32[]{:S(2)}) collective-permute-start(f32[1024,2,32]{0,2,1:T(8,128)} %get-tuple-element.561), channel_id=1, source_target_pairs={{0,4},{4,8},{8,12},{12,16},{16,20},{20,24},{24,28},{28,32},{32,36}... | collective-permute-start | bytes 786440 | tf_op jit(solution)/shard_map/while/body/eval_jaxpr/ppermute | solution.py:12
  96.1 10.6 collective-permute-start
  117.1 10.6 collective-permute-start
  138.1 10.6 collective-permute-start
  159.0 12.3 %collective-permute-start = (f32[1024,2,32]{0,2,1:T(8,128)}, f32[1024,2,32]{0,2,1:T(8,128)S(1)}, u32[]{:S(2)}, u32[]{:S(2)}) collective-permute-start(f32[1024,2,32]{0,2,1:T(8,128)} %get-tuple-element.561), channel_id=1, source_target_pairs={{0,4},{4,8},{8,12},{12,16},{16,20},{20,24},{24,28},{28,32},{32,36}... | collective-permute-start | bytes 786440 | tf_op jit(solution)/shard_map/while/body/eval_jaxpr/ppermute | solution.py:12
  171.3 13.6 %collective-permute-start = (f32[1024,2,32]{0,2,1:T(8,128)}, f32[1024,2,32]{0,2,1:T(8,128)S(1)}, u32[]{:S(2)}, u32[]{:S(2)}) collective-permute-start(f32[1024,2,32]{0,2,1:T(8,128)} %get-tuple-element.561), channel_id=1, source_target_pairs={{0,4},{4,8},{8,12},{12,16},{16,20},{20,24},{24,28},{28,32},{32,36}... | collective-permute-start | bytes 786440 | tf_op jit(solution)/shard_map/while/body/eval_jaxpr/ppermute | solution.py:12
  185.0 12.0 collective-permute-start
  196.9 13.1 %collective-permute-start = (f32[1024,2,32]{0,2,1:T(8,128)}, f32[1024,2,32]{0,2,1:T(8,128)S(1)}, u32[]{:S(2)}, u32[]{:S(2)}) collective-permute-start(f32[1024,2,32]{0,2,1:T(8,128)} %get-tuple-element.561), channel_id=1, source_target_pairs={{0,4},{4,8},{8,12},{12,16},{16,20},{20,24},{24,28},{28,32},{32,36}... | collective-permute-start | bytes 786440 | tf_op jit(solution)/shard_map/while/body/eval_jaxpr/ppermute | solution.py:12
  210.0 12.5 %collective-permute-start = (f32[1024,2,32]{0,2,1:T(8,128)}, f32[1024,2,32]{0,2,1:T(8,128)S(1)}, u32[]{:S(2)}, u32[]{:S(2)}) collective-permute-start(f32[1024,2,32]{0,2,1:T(8,128)} %get-tuple-element.561), channel_id=1, source_target_pairs={{0,4},{4,8},{8,12},{12,16},{16,20},{20,24},{24,28},{28,32},{32,36}... | collective-permute-start | bytes 786440 | tf_op jit(solution)/shard_map/while/body/eval_jaxpr/ppermute | solution.py:12
  222.6 11.7 collective-permute-start
  234.2 10.8 collective-permute-start
  245.1 21.4 %collective-permute-start = (f32[1024,2,32]{0,2,1:T(8,128)}, f32[1024,2,32]{0,2,1:T(8,128)S(1)}, u32[]{:S(2)}, u32[]{:S(2)}) collective-permute-start(f32[1024,2,32]{0,2,1:T(8,128)} %get-tuple-element.561), channel_id=1, source_target_pairs={{0,4},{4,8},{8,12},{12,16},{16,20},{20,24},{24,28},{28,32},{32,36}... | collective-permute-start | bytes 786440 | tf_op jit(solution)/shard_map/while/body/eval_jaxpr/ppermute | solution.py:12
  266.5 13.1 %collective-permute-start = (f32[1024,2,32]{0,2,1:T(8,128)}, f32[1024,2,32]{0,2,1:T(8,128)S(1)}, u32[]{:S(2)}, u32[]{:S(2)}) collective-permute-start(f32[1024,2,32]{0,2,1:T(8,128)} %get-tuple-element.561), channel_id=1, source_target_pairs={{0,4},{4,8},{8,12},{12,16},{16,20},{20,24},{24,28},{28,32},{32,36}... | collective-permute-start | bytes 786440 | tf_op jit(solution)/shard_map/while/body/eval_jaxpr/ppermute | solution.py:12
  279.5 11.5 collective-permute-start
  291.0 11.9 collective-permute-start
  302.9 11.7 collective-permute-start
  314.6 16.9 %collective-permute-start = (f32[1024,2,32]{0,2,1:T(8,128)}, f32[1024,2,32]{0,2,1:T(8,128)S(1)}, u32[]{:S(2)}, u32[]{:S(2)}) collective-permute-start(f32[1024,2,32]{0,2,1:T(8,128)} %get-tuple-element.561), channel_id=1, source_target_pairs={{0,4},{4,8},{8,12},{12,16},{16,20},{20,24},{24,28},{28,32},{32,36}... | collective-permute-start | bytes 786440 | tf_op jit(solution)/shard_map/while/body/eval_jaxpr/ppermute | solution.py:12
  331.6 11.5 collective-permute-start
  343.0 11.5 collective-permute-start
  354.5 12.2 %collective-permute-start = (f32[1024,2,32]{0,2,1:T(8,128)}, f32[1024,2,32]{0,2,1:T(8,128)S(1)}, u32[]{:S(2)}, u32[]{:S(2)}) collective-permute-start(f32[1024,2,32]{0,2,1:T(8,128)} %get-tuple-element.561), channel_id=1, source_target_pairs={{0,4},{4,8},{8,12},{12,16},{16,20},{20,24},{24,28},{28,32},{32,36}... | collective-permute-start | bytes 786440 | tf_op jit(solution)/shard_map/while/body/eval_jaxpr/ppermute | solution.py:12
  366.7 11.5 collective-permute-start
  378.2 13.6 %collective-permute-start = (f32[1024,2,32]{0,2,1:T(8,128)}, f32[1024,2,32]{0,2,1:T(8,128)S(1)}, u32[]{:S(2)}, u32[]{:S(2)}) collective-permute-start(f32[1024,2,32]{0,2,1:T(8,128)} %get-tuple-element.561), channel_id=1, source_target_pairs={{0,4},{4,8},{8,12},{12,16},{16,20},{20,24},{24,28},{28,32},{32,36}... | collective-permute-start | bytes 786440 | tf_op jit(solution)/shard_map/while/body/eval_jaxpr/ppermute | solution.py:12
  391.8 13.1 %collective-permute-start = (f32[1024,2,32]{0,2,1:T(8,128)}, f32[1024,2,32]{0,2,1:T(8,128)S(1)}, u32[]{:S(2)}, u32[]{:S(2)}) collective-permute-start(f32[1024,2,32]{0,2,1:T(8,128)} %get-tuple-element.561), channel_id=1, source_target_pairs={{0,4},{4,8},{8,12},{12,16},{16,20},{20,24},{24,28},{28,32},{32,36}... | collective-permute-start | bytes 786440 | tf_op jit(solution)/shard_map/while/body/eval_jaxpr/ppermute | solution.py:12
  404.9 13.2 %collective-permute-start = (f32[1024,2,32]{0,2,1:T(8,128)}, f32[1024,2,32]{0,2,1:T(8,128)S(1)}, u32[]{:S(2)}, u32[]{:S(2)}) collective-permute-start(f32[1024,2,32]{0,2,1:T(8,128)} %get-tuple-element.561), channel_id=1, source_target_pairs={{0,4},{4,8},{8,12},{12,16},{16,20},{20,24},{24,28},{28,32},{32,36}... | collective-permute-start | bytes 786440 | tf_op jit(solution)/shard_map/while/body/eval_jaxpr/ppermute | solution.py:12
  418.1 13.1 %collective-permute-start = (f32[1024,2,32]{0,2,1:T(8,128)}, f32[1024,2,32]{0,2,1:T(8,128)S(1)}, u32[]{:S(2)}, u32[]{:S(2)}) collective-permute-start(f32[1024,2,32]{0,2,1:T(8,128)} %get-tuple-element.561), channel_id=1, source_target_pairs={{0,4},{4,8},{8,12},{12,16},{16,20},{20,24},{24,28},{28,32},{32,36}... | collective-permute-start | bytes 786440 | tf_op jit(solution)/shard_map/while/body/eval_jaxpr/ppermute | solution.py:12
  431.2 21.5 %collective-permute-start = (f32[1024,2,32]{0,2,1:T(8,128)}, f32[1024,2,32]{0,2,1:T(8,128)S(1)}, u32[]{:S(2)}, u32[]{:S(2)}) collective-permute-start(f32[1024,2,32]{0,2,1:T(8,128)} %get-tuple-element.561), channel_id=1, source_target_pairs={{0,4},{4,8},{8,12},{12,16},{16,20},{20,24},{24,28},{28,32},{32,36}... | collective-permute-start | bytes 786440 | tf_op jit(solution)/shard_map/while/body/eval_jaxpr/ppermute | solution.py:12
  452.6 12.9 %collective-permute-start = (f32[1024,2,32]{0,2,1:T(8,128)}, f32[1024,2,32]{0,2,1:T(8,128)S(1)}, u32[]{:S(2)}, u32[]{:S(2)}) collective-permute-start(f32[1024,2,32]{0,2,1:T(8,128)} %get-tuple-element.561), channel_id=1, source_target_pairs={{0,4},{4,8},{8,12},{12,16},{16,20},{20,24},{24,28},{28,32},{32,36}... | collective-permute-start | bytes 786440 | tf_op jit(solution)/shard_map/while/body/eval_jaxpr/ppermute | solution.py:12
  465.5 14.3 %collective-permute-start = (f32[1024,2,32]{0,2,1:T(8,128)}, f32[1024,2,32]{0,2,1:T(8,128)S(1)}, u32[]{:S(2)}, u32[]{:S(2)}) collective-permute-start(f32[1024,2,32]{0,2,1:T(8,128)} %get-tuple-element.561), channel_id=1, source_target_pairs={{0,4},{4,8},{8,12},{12,16},{16,20},{20,24},{24,28},{28,32},{32,36}... | collective-permute-start | bytes 786440 | tf_op jit(solution)/shard_map/while/body/eval_jaxpr/ppermute | solution.py:12
  479.9 12.4 %collective-permute-start = (f32[1024,2,32]{0,2,1:T(8,128)}, f32[1024,2,32]{0,2,1:T(8,128)S(1)}, u32[]{:S(2)}, u32[]{:S(2)}) collective-permute-start(f32[1024,2,32]{0,2,1:T(8,128)} %get-tuple-element.561), channel_id=1, source_target_pairs={{0,4},{4,8},{8,12},{12,16},{16,20},{20,24},{24,28},{28,32},{32,36}... | collective-permute-start | bytes 786440 | tf_op jit(solution)/shard_map/while/body/eval_jaxpr/ppermute | solution.py:12
  492.2 19.7 %collective-permute-start = (f32[1024,2,32]{0,2,1:T(8,128)}, f32[1024,2,32]{0,2,1:T(8,128)S(1)}, u32[]{:S(2)}, u32[]{:S(2)}) collective-permute-start(f32[1024,2,32]{0,2,1:T(8,128)} %get-tuple-element.561), channel_id=1, source_target_pairs={{0,4},{4,8},{8,12},{12,16},{16,20},{20,24},{24,28},{28,32},{32,36}... | collective-permute-start | bytes 786440 | tf_op jit(solution)/shard_map/while/body/eval_jaxpr/ppermute | solution.py:12
  512.0 11.5 collective-permute-start
  523.6 13.0 %collective-permute-start.1 = (bf16[1024,2,32]{0,2,1:T(8,128)(2,1)S(1)}, bf16[1024,2,32]{0,2,1:T(8,128)(2,1)S(1)}, u32[]{:S(2)}, u32[]{:S(2)}) collective-permute-start(bf16[1024,2,32]{0,2,1:T(8,128)(2,1)S(1)} %get-tuple-element.591), channel_id=1, source_target_pairs={{4,0},{8,4},{12,8},{16,12},{20,16},{24,20},{28,24},{32,28},{36,32}... | collective-permute-start | bytes 393224 | tf_op jit(solution)/shard_map/while/body/eval_jaxpr/ppermute | solution.py:12
  536.6 11.6 collective-permute-start.1
  557.1 10.6 collective-permute-start.1
  577.1 9.9 collective-permute-start.1
  587.0 15.3 %collective-permute-start.1 = (bf16[1024,2,32]{0,2,1:T(8,128)(2,1)S(1)}, bf16[1024,2,32]{0,2,1:T(8,128)(2,1)S(1)}, u32[]{:S(2)}, u32[]{:S(2)}) collective-permute-start(bf16[1024,2,32]{0,2,1:T(8,128)(2,1)S(1)} %get-tuple-element.591), channel_id=1, source_target_pairs={{4,0},{8,4},{12,8},{16,12},{20,16},{24,20},{28,24},{32,28},{36,32}... | collective-permute-start | bytes 393224 | tf_op jit(solution)/shard_map/while/body/eval_jaxpr/ppermute | solution.py:12
  602.3 9.9 collective-permute-start.1
  612.2 14.5 %collective-permute-start.1 = (bf16[1024,2,32]{0,2,1:T(8,128)(2,1)S(1)}, bf16[1024,2,32]{0,2,1:T(8,128)(2,1)S(1)}, u32[]{:S(2)}, u32[]{:S(2)}) collective-permute-start(bf16[1024,2,32]{0,2,1:T(8,128)(2,1)S(1)} %get-tuple-element.591), channel_id=1, source_target_pairs={{4,0},{8,4},{12,8},{16,12},{20,16},{24,20},{28,24},{32,28},{36,32}... | collective-permute-start | bytes 393224 | tf_op jit(solution)/shard_map/while/body/eval_jaxpr/ppermute | solution.py:12
  626.7 12.7 %collective-permute-start.1 = (bf16[1024,2,32]{0,2,1:T(8,128)(2,1)S(1)}, bf16[1024,2,32]{0,2,1:T(8,128)(2,1)S(1)}, u32[]{:S(2)}, u32[]{:S(2)}) collective-permute-start(bf16[1024,2,32]{0,2,1:T(8,128)(2,1)S(1)} %get-tuple-element.591), channel_id=1, source_target_pairs={{4,0},{8,4},{12,8},{16,12},{20,16},{24,20},{28,24},{32,28},{36,32}... | collective-permute-start | bytes 393224 | tf_op jit(solution)/shard_map/while/body/eval_jaxpr/ppermute | solution.py:12
  639.4 12.4 %collective-permute-start.1 = (bf16[1024,2,32]{0,2,1:T(8,128)(2,1)S(1)}, bf16[1024,2,32]{0,2,1:T(8,128)(2,1)S(1)}, u32[]{:S(2)}, u32[]{:S(2)}) collective-permute-start(bf16[1024,2,32]{0,2,1:T(8,128)(2,1)S(1)} %get-tuple-element.591), channel_id=1, source_target_pairs={{4,0},{8,4},{12,8},{16,12},{20,16},{24,20},{28,24},{32,28},{36,32}... | collective-permute-start | bytes 393224 | tf_op jit(solution)/shard_map/while/body/eval_jaxpr/ppermute | solution.py:12
  651.8 12.0 collective-permute-start.1
  663.8 12.6 %collective-permute-start.1 = (bf16[1024,2,32]{0,2,1:T(8,128)(2,1)S(1)}, bf16[1024,2,32]{0,2,1:T(8,128)(2,1)S(1)}, u32[]{:S(2)}, u32[]{:S(2)}) collective-permute-start(bf16[1024,2,32]{0,2,1:T(8,128)(2,1)S(1)} %get-tuple-element.591), channel_id=1, source_target_pairs={{4,0},{8,4},{12,8},{16,12},{20,16},{24,20},{28,24},{32,28},{36,32}... | collective-permute-start | bytes 393224 | tf_op jit(solution)/shard_map/while/body/eval_jaxpr/ppermute | solution.py:12
  685.7 16.1 %collective-permute-start.1 = (bf16[1024,2,32]{0,2,1:T(8,128)(2,1)S(1)}, bf16[1024,2,32]{0,2,1:T(8,128)(2,1)S(1)}, u32[]{:S(2)}, u32[]{:S(2)}) collective-permute-start(bf16[1024,2,32]{0,2,1:T(8,128)(2,1)S(1)} %get-tuple-element.591), channel_id=1, source_target_pairs={{4,0},{8,4},{12,8},{16,12},{20,16},{24,20},{28,24},{32,28},{36,32}... | collective-permute-start | bytes 393224 | tf_op jit(solution)/shard_map/while/body/eval_jaxpr/ppermute | solution.py:12
  701.8 9.9 collective-permute-start.1
  711.6 15.1 %collective-permute-start.1 = (bf16[1024,2,32]{0,2,1:T(8,128)(2,1)S(1)}, bf16[1024,2,32]{0,2,1:T(8,128)(2,1)S(1)}, u32[]{:S(2)}, u32[]{:S(2)}) collective-permute-start(bf16[1024,2,32]{0,2,1:T(8,128)(2,1)S(1)} %get-tuple-element.591), channel_id=1, source_target_pairs={{4,0},{8,4},{12,8},{16,12},{20,16},{24,20},{28,24},{32,28},{36,32}... | collective-permute-start | bytes 393224 | tf_op jit(solution)/shard_map/while/body/eval_jaxpr/ppermute | solution.py:12
  726.8 9.5 collective-permute-start.1
  736.3 11.8 collective-permute-start.1
  757.3 15.5 %collective-permute-start.1 = (bf16[1024,2,32]{0,2,1:T(8,128)(2,1)S(1)}, bf16[1024,2,32]{0,2,1:T(8,128)(2,1)S(1)}, u32[]{:S(2)}, u32[]{:S(2)}) collective-permute-start(bf16[1024,2,32]{0,2,1:T(8,128)(2,1)S(1)} %get-tuple-element.591), channel_id=1, source_target_pairs={{4,0},{8,4},{12,8},{16,12},{20,16},{24,20},{28,24},{32,28},{36,32}... | collective-permute-start | bytes 393224 | tf_op jit(solution)/shard_map/while/body/eval_jaxpr/ppermute | solution.py:12
  772.8 9.9 collective-permute-start.1
  782.7 9.7 collective-permute-start.1
  792.4 9.9 collective-permute-start.1
  802.2 10.0 collective-permute-start.1
  812.2 9.9 collective-permute-start.1
  822.1 12.0 collective-permute-start.1
  834.1 268.4 %collective-permute-start.1 = (bf16[1024,2,32]{0,2,1:T(8,128)(2,1)S(1)}, bf16[1024,2,32]{0,2,1:T(8,128)(2,1)S(1)}, u32[]{:S(2)}, u32[]{:S(2)}) collective-permute-start(bf16[1024,2,32]{0,2,1:T(8,128)(2,1)S(1)} %get-tuple-element.591), channel_id=1, source_target_pairs={{4,0},{8,4},{12,8},{16,12},{20,16},{24,20},{28,24},{32,28},{36,32}... | collective-permute-start | bytes 393224 | tf_op jit(solution)/shard_map/while/body/eval_jaxpr/ppermute | solution.py:12
  1112.2 12.3 %collective-permute-start.1 = (bf16[1024,2,32]{0,2,1:T(8,128)(2,1)S(1)}, bf16[1024,2,32]{0,2,1:T(8,128)(2,1)S(1)}, u32[]{:S(2)}, u32[]{:S(2)}) collective-permute-start(bf16[1024,2,32]{0,2,1:T(8,128)(2,1)S(1)} %get-tuple-element.591), channel_id=1, source_target_pairs={{4,0},{8,4},{12,8},{16,12},{20,16},{24,20},{28,24},{32,28},{36,32}... | collective-permute-start | bytes 393224 | tf_op jit(solution)/shard_map/while/body/eval_jaxpr/ppermute | solution.py:12
  1134.1 9.6 collective-permute-start.1
  1153.4 9.7 collective-permute-start.1
  1179.6 16.2 %collective-permute-start.1 = (bf16[1024,2,32]{0,2,1:T(8,128)(2,1)S(1)}, bf16[1024,2,32]{0,2,1:T(8,128)(2,1)S(1)}, u32[]{:S(2)}, u32[]{:S(2)}) collective-permute-start(bf16[1024,2,32]{0,2,1:T(8,128)(2,1)S(1)} %get-tuple-element.591), channel_id=1, source_target_pairs={{4,0},{8,4},{12,8},{16,12},{20,16},{24,20},{28,24},{32,28},{36,32}... | collective-permute-start | bytes 393224 | tf_op jit(solution)/shard_map/while/body/eval_jaxpr/ppermute | solution.py:12
  1204.8 12.0 collective-permute-start.1
  (6 other events, 52.7 us)
where the time goes:
time: 1240 us; the launch traced here: 1220 us
  waiting for transfers between devices  794 us (64%)
  starting transfers between devices  338 us (27%)
  matrix products  75.2 us (6%)
    ppermute x70, waiting for transfers between devices, shifted(): lax.ppermute(value, axis, [(source, source + steps) for source in range(i...  794 us
    ppermute x70, starting transfers between devices, shifted(): lax.ppermute(value, axis, [(source, source + steps) for source in range(i...  338 us
    dot_general x16, matrix products, complex_apply(): jnp.dot(imag_part, merged, preferred_element_type=jnp.float32)  37.6 us
    dot_general x16, matrix products, complex_apply(): jnp.dot(real_part, merged, preferred_element_type=jnp.float32)  37.6 us
  transfers between devices with their start and end apart: 70, of which 70 were waited for; matrix products, arithmetic and copies ran while one was open for 0% of the time, Pallas kernels for 0%

commit v1 on v0

v1 whole, which is shorter than its diff:
```python
import functools

import jax
import jax.numpy as jnp
from jax import lax
from jax.experimental import pallas as pl
from jax.experimental.pallas import tpu as pltpu
from jax.sharding import PartitionSpec as P

GROUP = 4
BATCHES = 4
CHUNK = 64
LAG = 2
AXIS = "strip"
BF16 = jnp.bfloat16
F32 = jnp.float32
MIB = 2**20

VMEM = pl.BlockSpec(memory_space=pltpu.VMEM)
SMEM = pl.BlockSpec(memory_space=pltpu.SMEM)
ANY = pl.BlockSpec(memory_space=pl.ANY)


def multiply(rows, matrix):
    real, imag = rows[0], rows[1]
    size = real.shape[-1]
    direct = jnp.concatenate([real, imag], axis=0)
    crossed = jnp.concatenate([-imag, real], axis=0)
    return jnp.dot(direct, matrix[0, :size, :], preferred_element_type=F32) + jnp.dot(
        crossed, matrix[1, :size, :], preferred_element_type=F32
    )


def halves(value):
    return value.reshape(2, value.shape[0] // 2, value.shape[1])


def call(kernel, outs, specs_in, specs_out, *operands, scratch=(), aliases=None, rows=32, times=1, limit=24):
    size = 1024
    return pl.pallas_call(
        kernel,
        out_shape=outs,
        in_specs=specs_in,
        out_specs=specs_out,
        scratch_shapes=scratch,
        input_output_aliases=aliases or {},
        compiler_params=pltpu.CompilerParams(vmem_limit_bytes=limit * MIB),
        cost_estimate=pl.CostEstimate(
            flops=8 * times * rows * size * size, bytes_accessed=4 * times * size * size, transcendentals=0
        ),
    )(*operands)


def sweep_kernel(aliased, flags, block, first, second, add_first, add_second, *refs):
    own, got, out, work, sems = refs[2:] if aliased else refs
    mode, row, extra = flags[0], flags[1], flags[2]
    chunk = block.shape[1]

    @pl.when(mode == 1)
    def _():
        for part in range(2):
            work[part] = first[part, pl.ds(pl.multiple_of(row, chunk), chunk), :]

    @pl.when(mode == 2)
    def _():
        place = pl.ds(pl.multiple_of(extra, chunk), chunk)
        entered = (block[...].astype(F32) + add_first[:, place, :].astype(F32)).astype(BF16)
        work[...] = (halves(multiply(entered, first)) + add_second[:, place, :].astype(F32)).astype(BF16)

    @pl.when(mode > 0)
    def _():
        place = pl.ds(pl.multiple_of(row, chunk), chunk)
        keep = pltpu.make_async_copy(block, got.at[:, place, :], sems.at[0])
        keep.start()
        out[...] = halves(multiply(work[...], second)).astype(BF16)
        store = pltpu.make_async_copy(out, own.at[:, place, :], sems.at[1])
        store.start()
        keep.wait()
        store.wait()


def sweep(flags, block, first, second, add_first, add_second, kept):
    chunk, size = block.shape[1:]
    length = size + add_first.shape[1] - chunk
    buffer = jax.ShapeDtypeStruct((2, length, size), BF16)
    return call(
        functools.partial(sweep_kernel, kept is not None),
        (buffer, buffer, jax.ShapeDtypeStruct(block.shape, BF16)),
        [SMEM] + [VMEM] * 5 + ([ANY, ANY] if kept else []),
        (ANY, ANY, VMEM),
        flags,
        block,
        first,
        second,
        add_first,
        add_second,
        *(kept or ()),
        scratch=[pltpu.VMEM(block.shape, BF16), pltpu.SemaphoreType.DMA((2,))],
        aliases={6: 0, 7: 1} if kept else None,
        rows=chunk,
        times=2,
    )


def chain_kernel(block, matrix, constant, out):
    out[...] = (halves(multiply(block[...], matrix)) + constant[...].astype(F32)).astype(BF16)


def chain(block, matrix, constant):
    return call(
        chain_kernel, jax.ShapeDtypeStruct(block.shape, BF16), [VMEM] * 3, VMEM, block, matrix, constant
    )


def trace_kernel(flags, entry, before, source, first, second, trace_first, trace_second, enter):
    size = entry.shape[2]

    @pl.when(flags[0] == 0)
    def _():
        enter[...] = entry[...].astype(F32)

    @pl.when(flags[0] != 0)
    def _():
        enter[...] = halves(multiply(entry[...], before)) + before[:, size:, :].astype(F32)

    one = halves(multiply((source[0].astype(F32) + enter[...]).astype(BF16), first))
    trace_first[...] = one
    trace_second[...] = halves(multiply((source[1].astype(F32) + one).astype(BF16), second))


def inner_kernel(block, first, second, trace_first, trace_second, out):
    middle = (trace_second[...] + halves(multiply(block[...], second))).astype(BF16)
    out[...] = (trace_first[...] + halves(multiply(middle, first))).astype(BF16)


def field_kernel(flags, entry, after, constant, first, second, trace_first, trace_second, out, enter):
    @pl.when(flags[0] == 0)
    def _():
        enter[...] = entry[...]

    @pl.when(flags[0] != 0)
    def _():
        enter[...] = (halves(multiply(entry[...], after)) + constant[...].astype(F32)).astype(BF16)

    field = (trace_second[...] + halves(multiply(enter[...], second))).astype(BF16)
    out[1] = field
    out[0] = (trace_first[...] + halves(multiply(field, first))).astype(BF16)


def take(buffer, index):
    return lax.dynamic_index_in_dim(buffer, index, 0, keepdims=False)


def put(buffer, value, index):
    return lax.dynamic_update_index_in_dim(buffer, value, index, 0)


def slot(index, count):
    return jnp.where(jnp.logical_and(index >= 0, index < count), index, count)


def shards(source, pivot_inverse_real, factor_imag):
    strips = lax.axis_size(AXIS)
    groups = strips // GROUP
    position = lax.axis_index(AXIS)
    group = position // GROUP
    place = position % GROUP
    mirror = GROUP - 1 - place
    size = source.shape[1]
    columns = source.shape[3]
    width = columns // BATCHES
    chunks = size // CHUNK
    total = (size + columns) // CHUNK

    vectors = source.transpose(0, 2, 3, 1)
    first, second = (
        jnp.stack([pivot_inverse_real[layer].T, factor_imag[layer].T]) for layer in range(2)
    )

    add_first, add_second = (jnp.pad(vectors[layer], ((0, 0), (CHUNK, 0), (0, 0))) for layer in range(2))
    nothing = jnp.zeros((2, CHUNK, size), BF16)
    up = [(s, s + 1) for s in range(strips) if s % GROUP != GROUP - 1]
    down = [(s + 1, s) for s, _ in up]

    def moved(outs, step, pairs, count):
        live = [
            (s, d)
            for s, d in pairs
            if 0 <= step - LAG * (s % GROUP if d > s else GROUP - 1 - s % GROUP) < count
        ]
        return lax.ppermute(outs[step - LAG], AXIS, live)

    def flags_of(step, rank, count):
        index = step - LAG * (rank - 1)
        valid = jnp.logical_and(index >= 0, index < count)
        mode = jnp.where(jnp.logical_and(rank == 0, index < chunks), 1, 2)
        return jnp.stack(
            [
                jnp.where(valid, mode, 0),
                jnp.clip(index, 0, count - 1) * CHUNK,
                jnp.clip(index - chunks + 1, 0, total - chunks) * CHUNK,
            ]
        ).astype(jnp.int32)

    outs_f, outs_b = {}, {}
    kept_f = kept_b = None
    for step in range(-LAG, total + LAG * (GROUP - 2)):
        block = moved(outs_f, step, up, total) if step >= 0 else nothing
        *kept_f, outs_f[step] = sweep(
            flags_of(step, place, total), block, first, second, add_first, add_second, kept_f
        )
        if step < chunks + LAG * (GROUP - 2):
            block = moved(outs_b, step, down, chunks) if step >= 0 else nothing
            *kept_b, outs_b[step] = sweep(
                flags_of(step, mirror, chunks), block, second, first, nothing, nothing, kept_b
            )
    prefix, prefix_before = kept_f
    suffix, suffix_after = kept_b

    def joined(value):
        return value[:BATCHES].swapaxes(0, 1).reshape(2, columns, size)

    nought = jnp.zeros((2, width, size), BF16)
    blocks = jnp.zeros((BATCHES + 1, 2, width, size), BF16)
    incoming = sent = blocks
    block = nought
    for moment in range(groups - 2 + BATCHES):
        index = slot(moment - group, BATCHES)
        start = size + jnp.minimum(index, BATCHES - 1) * width
        constant = lax.dynamic_slice_in_dim(prefix, start, width, 1)
        outgoing = chain(block, prefix, constant)
        sent = put(sent, outgoing, index)
        pairs = [
            (GROUP * g + GROUP - 1, GROUP * g + 2 * GROUP - 1)
            for g in range(groups - 1)
            if 0 <= moment - g < BATCHES
        ]
        block = lax.ppermute(outgoing, AXIS, pairs)
        incoming = put(incoming, block, slot(moment - group + 1, BATCHES))
    whole = joined(sent)
    entry = jnp.where(jnp.logical_and(place == GROUP - 1, group > 0), joined(incoming), 0)
    for other in range(GROUP - 1):
        entry += lax.ppermute(
            whole,
            AXIS,
            [(GROUP * g + GROUP - 1, GROUP * g + GROUP + other) for g in range(groups - 1)],
        )

    trace = jax.ShapeDtypeStruct((2, columns, size), F32)
    trace_first, trace_second = call(
        trace_kernel,
        (trace, trace),
        [SMEM] + [VMEM] * 5,
        (VMEM, VMEM),
        place[None].astype(jnp.int32),
        entry,
        prefix_before,
        vectors,
        first,
        second,
        scratch=[pltpu.VMEM((2, columns, size), F32)],
        rows=columns,
        times=3,
        limit=32,
    )

    inner = inner_sent = blocks
    block = nought
    for moment in range(GROUP - 1 + BATCHES):
        index = slot(moment - mirror, BATCHES)
        start = jnp.minimum(index, BATCHES - 1) * width
        outgoing = call(
            inner_kernel,
            jax.ShapeDtypeStruct(block.shape, BF16),
            [VMEM] * 5,
            VMEM,
            block,
            first,
            second,
            lax.dynamic_slice_in_dim(trace_first, start, width, 1),
            lax.dynamic_slice_in_dim(trace_second, start, width, 1),
            times=2,
        )
        inner_sent = put(inner_sent, outgoing, index)
        pairs = [(s, d) for s, d in down if 0 <= moment - (GROUP - 1 - s % GROUP) < BATCHES]
        if pairs:
            block = lax.ppermute(outgoing, AXIS, pairs)
            inner = put(inner, block, slot(moment - mirror + 1, BATCHES))
    incoming = sent = blocks
    block = nought
    far = groups - 1 - group
    for moment in range(groups - 2 + BATCHES):
        index = slot(moment - far, BATCHES)
        outgoing = chain(block, suffix, take(inner_sent, index))
        sent = put(sent, outgoing, index)
        pairs = [
            (GROUP * g + GROUP, GROUP * g)
            for g in range(groups - 1)
            if 0 <= moment - (groups - 2 - g) < BATCHES
        ]
        block = lax.ppermute(outgoing, AXIS, pairs)
        incoming = put(incoming, block, slot(moment - far + 1, BATCHES))
    whole = joined(sent)
    entry = jnp.where(jnp.logical_and(place == 0, far > 0), joined(incoming), 0)
    for other in range(1, GROUP):
        entry += lax.ppermute(
            whole, AXIS, [(GROUP * g + GROUP, GROUP * g + other) for g in range(groups - 1)]
        )
    fields = call(
        field_kernel,
        jax.ShapeDtypeStruct((2, 2, columns, size), BF16),
        [SMEM] + [VMEM] * 7,
        VMEM,
        mirror[None].astype(jnp.int32),
        entry,
        suffix_after,
        joined(inner),
        first,
        second,
        trace_first,
        trace_second,
        scratch=[pltpu.VMEM((2, columns, size), BF16)],
        rows=columns,
        times=3,
        limit=32,
    )
    return fields.transpose(0, 3, 1, 2)


def solution(mesh):
    placed = (P("strip", None, None, "wave"), P("strip", "wave", None), P("strip", "wave", None))
    return jax.shard_map(
        shards,
        mesh=mesh,
        in_specs=placed,
        out_specs=P("strip", None, None, "wave"),
        check_vma=False,
    )
```

time: 1240 us -> 633 us (0.51)
  waiting for transfers between devices: 794 us -> 169 us
  Pallas kernels: 0 us -> 107 us
  starting transfers between devices: 338 us -> 232 us
  local copies, waits for them, and re-layouts: 5.54 us -> 99.9 us
  matrix products: 75.2 us -> 0 us
    ppermute x70 -> x74, waiting for transfers between devices: 794 us -> 169 us  [the longest x26 126 us: shards(): block = lax.ppermute(outgoing, AXIS, pairs)]
    pallas_call x0 -> x75, Pallas kernels: none -> 107 us  [call(): pl.pallas_call(kernel, out_shape=outs, in_specs=specs_in, out_specs=specs...]
    ppermute x70 -> x74, starting transfers between devices: 338 us -> 232 us  [the longest x42 200 us: moved(): return lax.ppermute(outs[step - LAG], AXIS, live)]
    unnamed x0 -> x97, local copies, waits for them, and re-layouts: none -> 86.8 us
    dot_general x32 -> x0, matrix products: 75.2 us -> none  [the longest x16 37.6 us: complex_apply(): jnp.dot(imag_part, merged, preferred_element_type=jnp.float32)]
  transfers between devices with their start and end apart: 70 -> 74, of which waited for: 70 -> 11; matrix products, arithmetic and copies ran while one was open for 0% -> 1% of each run, Pallas kernels for 0% -> 11%
where the time goes in v1:
time: 633 us; the launch traced here: 621 us
  starting transfers between devices  232 us (37%)
  waiting for transfers between devices  169 us (27%)
  Pallas kernels  107 us (17%)
  local copies, waits for them, and re-layouts  99.9 us (16%)
  other arithmetic  7.57 us (1%)
    ppermute x42, starting transfers between devices, moved(): return lax.ppermute(outs[step - LAG], AXIS, live)  200 us
    ppermute x26, waiting for transfers between devices, shards(): block = lax.ppermute(outgoing, AXIS, pairs)  126 us
    pallas_call x75, Pallas kernels, call(): pl.pallas_call(kernel, out_shape=outs, in_specs=specs_in, out_specs=specs...  107 us
    unnamed x97, local copies, waits for them, and re-layouts  86.8 us
    ppermute x3, waiting for transfers between devices, shards(): lax.ppermute(whole, AXIS, [(GROUP * g + GROUP - 1, GROUP * g + GROUP + ot...  33.1 us
    ppermute x26, starting transfers between devices, shards(): block = lax.ppermute(outgoing, AXIS, pairs)  25.5 us
  transfers between devices with their start and end apart: 74, of which 11 were waited for; matrix products, arithmetic and copies ran while one was open for 1% of the time, Pallas kernels for 11%

profile of v1, /device:TPU:8, one launch (start us, length us, event | category | flops | bytes accessed | tf_op | source)
XLA Modules:
  0.0 621.2 jit_solution(1744162145607076395)
XLA Ops:
  0.0 4.0 fusion.4
  4.0 3.9 copy.151
  8.0 4.7 fusion.5
  12.6 3.9 copy.152
  16.6 2.6 copy.153
  19.1 4.0 copy.154
  25.1 3.8 pad_maximum_fusion
  29.0 2.7 shard_map.59
  31.7 2.5 collective-permute-start.21
  47.1 7.9 %collective-permute-start.1 = (bf16[2,64,1024]{2,1,0:T(8,128)(2,1)}, bf16[2,64,1024]{2,1,0:T(8,128)(2,1)S(1)}, u32[]{:S(2)}, u32[]{:S(2)}) collective-permute-start(bf16[2,64,1024]{2,1,0:T(8,128)(2,1)} %get-tuple-element.144), channel_id=1, source_target_pairs={{12,8},{28,24},{44,40},{60,56},{76,72},{92,88},{108,104},{124,120}... | collective-permute-start | bytes 786440 | tf_op jit(solution)/shard_map/ppermute | solution.py:191
  70.6 2.3 copy-done.11
  73.0 2.3 copy-done.16
  76.9 11.2 %collective-permute-start.23 = (bf16[2,64,1024]{2,1,0:T(8,128)(2,1)S(1)}, bf16[2,64,1024]{2,1,0:T(8,128)(2,1)S(1)}, u32[]{:S(2)}, u32[]{:S(2)}) collective-permute-start(bf16[2,64,1024]{2,1,0:T(8,128)(2,1)S(1)} %get-tuple-element.213), channel_id=1, source_target_pairs={{0,4},{4,8},{16,20},{20,24},{32,36},{36,40},{48,52},{52,56},{64,68... | collective-permute-start | bytes 786440 | tf_op jit(solution)/shard_map/ppermute | solution.py:191
  89.5 2.4 copy-done.12
  91.9 2.4 copy-done.17
  94.3 9.5 %collective-permute-start.22 = (bf16[2,64,1024]{2,1,0:T(8,128)(2,1)S(1)}, bf16[2,64,1024]{2,1,0:T(8,128)(2,1)S(1)}, u32[]{:S(2)}, u32[]{:S(2)}) collective-permute-start(bf16[2,64,1024]{2,1,0:T(8,128)(2,1)S(1)} %get-tuple-element.212), channel_id=1, source_target_pairs={{0,4},{4,8},{16,20},{20,24},{32,36},{36,40},{48,52},{52,56},{64,68... | collective-permute-start | bytes 786440 | tf_op jit(solution)/shard_map/ppermute | solution.py:191
  104.4 10.4 %collective-permute-start.3 = (bf16[2,64,1024]{2,1,0:T(8,128)(2,1)S(1)}, bf16[2,64,1024]{2,1,0:T(8,128)(2,1)S(1)}, u32[]{:S(2)}, u32[]{:S(2)}) collective-permute-start(bf16[2,64,1024]{2,1,0:T(8,128)(2,1)S(1)} %get-tuple-element.150), channel_id=1, source_target_pairs={{8,4},{12,8},{24,20},{28,24},{40,36},{44,40},{56,52},{60,56},{72,6... | collective-permute-start | bytes 786440 | tf_op jit(solution)/shard_map/ppermute | solution.py:191
  116.1 2.3 copy-done.18
  119.8 4.7 collective-permute-start.25
  128.1 6.9 %collective-permute-start.24 = (bf16[2,64,1024]{2,1,0:T(8,128)(2,1)S(1)}, bf16[2,64,1024]{2,1,0:T(8,128)(2,1)S(1)}, u32[]{:S(2)}, u32[]{:S(2)}) collective-permute-start(bf16[2,64,1024]{2,1,0:T(8,128)(2,1)S(1)} %get-tuple-element.218), channel_id=1, source_target_pairs={{0,4},{4,8},{8,12},{16,20},{20,24},{24,28},{32,36},{36,40},{40,44}... | collective-permute-start | bytes 786440 | tf_op jit(solution)/shard_map/ppermute | solution.py:191
  138.8 2.3 copy-done.20
  142.5 7.4 %collective-permute-start.27 = (bf16[2,64,1024]{2,1,0:T(8,128)(2,1)S(1)}, bf16[2,64,1024]{2,1,0:T(8,128)(2,1)S(1)}, u32[]{:S(2)}, u32[]{:S(2)}) collective-permute-start(bf16[2,64,1024]{2,1,0:T(8,128)(2,1)S(1)} %get-tuple-element.225), channel_id=1, source_target_pairs={{0,4},{4,8},{8,12},{16,20},{20,24},{24,28},{32,36},{36,40},{40,44}... | collective-permute-start | bytes 786440 | tf_op jit(solution)/shard_map/ppermute | solution.py:191
  153.8 4.6 collective-permute-start.26
  165.3 2.3 copy-done.22
  169.0 5.9 collective-permute-start.29
  178.4 4.6 collective-permute-start.28
  189.9 2.3 copy-done.24
  193.6 5.9 collective-permute-start.31
  203.0 4.8 collective-permute-start.30
  214.6 2.3 copy-done.26
  218.4 5.9 collective-permute-start.33
  227.8 4.6 collective-permute-start.32
  239.3 2.3 copy-done.28
  243.0 5.9 collective-permute-start.35
  252.4 4.6 collective-permute-start.34
  257.1 2.3 shard_map.51
  264.1 2.3 copy-done.30
  268.5 5.2 collective-permute-start.37
  278.0 3.9 collective-permute-start.36
  284.0 8.7 %collective-permute-start.17 = (bf16[2,64,1024]{2,1,0:T(8,128)(2,1)S(1)}, bf16[2,64,1024]{2,1,0:T(8,128)(2,1)S(1)}, u32[]{:S(2)}, u32[]{:S(2)}) collective-permute-start(bf16[2,64,1024]{2,1,0:T(8,128)(2,1)S(1)} %get-tuple-element.192), channel_id=1, source_target_pairs={{4,0},{8,4},{20,16},{24,20},{36,32},{40,36},{52,48},{56,52},{68,64... | collective-permute-start | bytes 786440 | tf_op jit(solution)/shard_map/ppermute | solution.py:191
  296.1 2.3 copy-done.32
  299.0 12.9 %collective-permute-start.39 = (bf16[2,64,1024]{2,1,0:T(8,128)(2,1)S(1)}, bf16[2,64,1024]{2,1,0:T(8,128)(2,1)S(1)}, u32[]{:S(2)}, u32[]{:S(2)}) collective-permute-start(bf16[2,64,1024]{2,1,0:T(8,128)(2,1)S(1)} %get-tuple-element.261), channel_id=1, source_target_pairs={{4,8},{8,12},{20,24},{24,28},{36,40},{40,44},{52,56},{56,60},{68,7... | collective-permute-start | bytes 786440 | tf_op jit(solution)/shard_map/ppermute | solution.py:191
  314.6 11.7 %collective-permute-start.38 = (bf16[2,64,1024]{2,1,0:T(8,128)(2,1)S(1)}, bf16[2,64,1024]{2,1,0:T(8,128)(2,1)S(1)}, u32[]{:S(2)}, u32[]{:S(2)}) collective-permute-start(bf16[2,64,1024]{2,1,0:T(8,128)(2,1)S(1)} %get-tuple-element.260), channel_id=1, source_target_pairs={{4,8},{8,12},{20,24},{24,28},{36,40},{40,44},{52,56},{56,60},{68,7... | collective-permute-start | bytes 786440 | tf_op jit(solution)/shard_map/ppermute | solution.py:191
  328.4 8.7 %collective-permute-start.19 = (bf16[2,64,1024]{2,1,0:T(8,128)(2,1)S(1)}, bf16[2,64,1024]{2,1,0:T(8,128)(2,1)S(1)}, u32[]{:S(2)}, u32[]{:S(2)}) collective-permute-start(bf16[2,64,1024]{2,1,0:T(8,128)(2,1)S(1)} %get-tuple-element.198), channel_id=1, source_target_pairs={{4,0},{20,16},{36,32},{52,48},{68,64},{84,80},{100,96},{116,112},{... | collective-permute-start | bytes 786440 | tf_op jit(solution)/shard_map/ppermute | solution.py:191
  337.1 2.5 shard_map.56
  340.9 2.3 copy-done.34
  343.8 9.2 %collective-permute-start.41 = (bf16[2,64,1024]{2,1,0:T(8,128)(2,1)S(1)}, bf16[2,64,1024]{2,1,0:T(8,128)(2,1)S(1)}, u32[]{:S(2)}, u32[]{:S(2)}) collective-permute-start(bf16[2,64,1024]{2,1,0:T(8,128)(2,1)S(1)} %get-tuple-element.267), channel_id=1, source_target_pairs={{8,12},{24,28},{40,44},{56,60},{72,76},{88,92},{104,108},{120,124}... | collective-permute-start | bytes 786440 | tf_op jit(solution)/shard_map/ppermute | solution.py:191
  355.8 11.7 %collective-permute-start.40 = (bf16[2,64,1024]{2,1,0:T(8,128)(2,1)S(1)}, bf16[2,64,1024]{2,1,0:T(8,128)(2,1)S(1)}, u32[]{:S(2)}, u32[]{:S(2)}) collective-permute-start(bf16[2,64,1024]{2,1,0:T(8,128)(2,1)S(1)} %get-tuple-element.266), channel_id=1, source_target_pairs={{8,12},{24,28},{40,44},{56,60},{72,76},{88,92},{104,108},{120,124}... | collective-permute-start | bytes 786440 | tf_op jit(solution)/shard_map/ppermute | solution.py:191
  367.5 2.8 shard_map.57
  370.2 2.8 shard_map.58
  373.1 3.8 copy-done.36
  398.8 33.1 %collective-permute-done.52 = bf16[2,128,1024]{2,1,0:T(8,128)(2,1)S(1)} collective-permute-done((bf16[2,128,1024]{2,1,0:T(8,128)(2,1)S(1)}, bf16[2,128,1024]{2,1,0:T(8,128)(2,1)S(1)}, u32[]{:S(2)}, u32[]{:S(2)}) %collective-permute-start.52) | collective-permute-done | bytes 524320 | tf_op jit(solution)/shard_map/ppermute | solution.py:243
  432.1 2.5 shard_map.93
  443.0 34.0 %collective-permute-done.57.block = bf16[2,32,1024]{2,1,0:T(8,128)(2,1)S(1)} collective-permute-done((bf16[2,32,1024]{2,1,0:T(8,128)(2,1)S(1)}, bf16[2,32,1024]{2,1,0:T(8,128)(2,1)S(1)}, u32[]{:S(2)}, u32[]{:S(2)}) %collective-permute-start.57) | collective-permute-done | bytes 131104 | tf_op jit(solution)/shard_map/ppermute | solution.py:287
  479.9 5.9 collective-permute-done.58.block
  488.8 5.5 collective-permute-done.59.block
  497.3 5.5 collective-permute-done.60.block
  514.9 57.8 %collective-permute-done.66.block = bf16[2,32,1024]{2,1,0:T(8,128)(2,1)S(1)} collective-permute-done((bf16[2,32,1024]{2,1,0:T(8,128)(2,1)S(1)}, bf16[2,32,1024]{2,1,0:T(8,128)(2,1)S(1)}, u32[]{:S(2)}, u32[]{:S(2)}) %collective-permute-start.66) | collective-permute-done | bytes 131104 | tf_op jit(solution)/shard_map/ppermute | solution.py:301
  575.6 5.8 collective-permute-done.67.block
  584.2 5.8 collective-permute-done.68.block
  592.8 5.8 collective-permute-done.69.block
  605.0 3.9 collective-permute-done.71
  608.9 5.6 collective-permute-done.72
  614.7 4.0 shard_map.111
  (380 shorter events, 187.4 us)
Async XLA Ops:
  31.7 34.5 %collective-permute-start.21 = (bf16[2,64,1024]{2,1,0:T(8,128)(2,1)}, bf16[2,64,1024]{2,1,0:T(8,128)(2,1)S(1)}, u32[]{:S(2)}, u32[]{:S(2)}) collective-permute-start(bf16[2,64,1024]{2,1,0:T(8,128)(2,1)} %get-tuple-element.207), channel_id=1, source_target_pairs={{0,4},{16,20},{32,36},{48,52},{64,68},{80,84},{96,100},{112,116},{... | collective-permute-start | bytes 786440 | tf_op jit(solution)/shard_map/ppermute | solution.py:191
  39.9 48.1 %collective-permute-start.20 = (bf16[2,64,1024]{2,1,0:T(8,128)(2,1)S(1)}, bf16[2,64,1024]{2,1,0:T(8,128)(2,1)S(1)}, u32[]{:S(2)}, u32[]{:S(2)}) collective-permute-start(bf16[2,64,1024]{2,1,0:T(8,128)(2,1)S(1)} %get-tuple-element.206), channel_id=1, source_target_pairs={{0,4},{16,20},{32,36},{48,52},{64,68},{80,84},{96,100},{112,116},{... | collective-permute-start | bytes 786440 | tf_op jit(solution)/shard_map/ppermute | solution.py:191
  47.1 56.7 %collective-permute-start.1 = (bf16[2,64,1024]{2,1,0:T(8,128)(2,1)}, bf16[2,64,1024]{2,1,0:T(8,128)(2,1)S(1)}, u32[]{:S(2)}, u32[]{:S(2)}) collective-permute-start(bf16[2,64,1024]{2,1,0:T(8,128)(2,1)} %get-tuple-element.144), channel_id=1, source_target_pairs={{12,8},{28,24},{44,40},{60,56},{76,72},{92,88},{108,104},{124,120}... | collective-permute-start | bytes 786440 | tf_op jit(solution)/shard_map/ppermute | solution.py:191
  60.2 54.6 %collective-permute-start = (bf16[2,64,1024]{2,1,0:T(8,128)(2,1)}, bf16[2,64,1024]{2,1,0:T(8,128)(2,1)S(1)}, u32[]{:S(2)}, u32[]{:S(2)}) collective-permute-start(bf16[2,64,1024]{2,1,0:T(8,128)(2,1)} %get-tuple-element.143), channel_id=1, source_target_pairs={{12,8},{28,24},{44,40},{60,56},{76,72},{92,88},{108,104},{124,120}... | collective-permute-start | bytes 786440 | tf_op jit(solution)/shard_map/ppermute | solution.py:191
  76.9 39.2 %collective-permute-start.23 = (bf16[2,64,1024]{2,1,0:T(8,128)(2,1)S(1)}, bf16[2,64,1024]{2,1,0:T(8,128)(2,1)S(1)}, u32[]{:S(2)}, u32[]{:S(2)}) collective-permute-start(bf16[2,64,1024]{2,1,0:T(8,128)(2,1)S(1)} %get-tuple-element.213), channel_id=1, source_target_pairs={{0,4},{4,8},{16,20},{20,24},{32,36},{36,40},{48,52},{52,56},{64,68... | collective-permute-start | bytes 786440 | tf_op jit(solution)/shard_map/ppermute | solution.py:191
  94.3 30.2 %collective-permute-start.22 = (bf16[2,64,1024]{2,1,0:T(8,128)(2,1)S(1)}, bf16[2,64,1024]{2,1,0:T(8,128)(2,1)S(1)}, u32[]{:S(2)}, u32[]{:S(2)}) collective-permute-start(bf16[2,64,1024]{2,1,0:T(8,128)(2,1)S(1)} %get-tuple-element.212), channel_id=1, source_target_pairs={{0,4},{4,8},{16,20},{20,24},{32,36},{36,40},{48,52},{52,56},{64,68... | collective-permute-start | bytes 786440 | tf_op jit(solution)/shard_map/ppermute | solution.py:191
  104.4 30.5 %collective-permute-start.3 = (bf16[2,64,1024]{2,1,0:T(8,128)(2,1)S(1)}, bf16[2,64,1024]{2,1,0:T(8,128)(2,1)S(1)}, u32[]{:S(2)}, u32[]{:S(2)}) collective-permute-start(bf16[2,64,1024]{2,1,0:T(8,128)(2,1)S(1)} %get-tuple-element.150), channel_id=1, source_target_pairs={{8,4},{12,8},{24,20},{28,24},{40,36},{44,40},{56,52},{60,56},{72,6... | collective-permute-start | bytes 786440 | tf_op jit(solution)/shard_map/ppermute | solution.py:191
  115.4 21.4 %collective-permute-start.2 = (bf16[2,64,1024]{2,1,0:T(8,128)(2,1)S(1)}, bf16[2,64,1024]{2,1,0:T(8,128)(2,1)S(1)}, u32[]{:S(2)}, u32[]{:S(2)}) collective-permute-start(bf16[2,64,1024]{2,1,0:T(8,128)(2,1)S(1)} %get-tuple-element.149), channel_id=1, source_target_pairs={{8,4},{12,8},{24,20},{28,24},{40,36},{44,40},{56,52},{60,56},{72,6... | collective-permute-start | bytes 786440 | tf_op jit(solution)/shard_map/ppermute | solution.py:191
  119.8 18.9 %collective-permute-start.25 = (bf16[2,64,1024]{2,1,0:T(8,128)(2,1)S(1)}, bf16[2,64,1024]{2,1,0:T(8,128)(2,1)S(1)}, u32[]{:S(2)}, u32[]{:S(2)}) collective-permute-start(bf16[2,64,1024]{2,1,0:T(8,128)(2,1)S(1)} %get-tuple-element.219), channel_id=1, source_target_pairs={{0,4},{4,8},{8,12},{16,20},{20,24},{24,28},{32,36},{36,40},{40,44}... | collective-permute-start | bytes 786440 | tf_op jit(solution)/shard_map/ppermute | solution.py:191
  128.1 21.8 %collective-permute-start.24 = (bf16[2,64,1024]{2,1,0:T(8,128)(2,1)S(1)}, bf16[2,64,1024]{2,1,0:T(8,128)(2,1)S(1)}, u32[]{:S(2)}, u32[]{:S(2)}) collective-permute-start(bf16[2,64,1024]{2,1,0:T(8,128)(2,1)S(1)} %get-tuple-element.218), channel_id=1, source_target_pairs={{0,4},{4,8},{8,12},{16,20},{20,24},{24,28},{32,36},{36,40},{40,44}... | collective-permute-start | bytes 786440 | tf_op jit(solution)/shard_map/ppermute | solution.py:191
  135.5 22.9 %collective-permute-start.5 = (bf16[2,64,1024]{2,1,0:T(8,128)(2,1)S(1)}, bf16[2,64,1024]{2,1,0:T(8,128)(2,1)S(1)}, u32[]{:S(2)}, u32[]{:S(2)}) collective-permute-start(bf16[2,64,1024]{2,1,0:T(8,128)(2,1)S(1)} %get-tuple-element.156), channel_id=1, source_target_pairs={{4,0},{8,4},{12,8},{20,16},{24,20},{28,24},{36,32},{40,36},{44,40}... | collective-permute-start | bytes 786440 | tf_op jit(solution)/shard_map/ppermute | solution.py:191
  137.4 24.4 %collective-permute-start.4 = (bf16[2,64,1024]{2,1,0:T(8,128)(2,1)S(1)}, bf16[2,64,1024]{2,1,0:T(8,128)(2,1)S(1)}, u32[]{:S(2)}, u32[]{:S(2)}) collective-permute-start(bf16[2,64,1024]{2,1,0:T(8,128)(2,1)S(1)} %get-tuple-element.155), channel_id=1, source_target_pairs={{4,0},{8,4},{12,8},{20,16},{24,20},{28,24},{36,32},{40,36},{44,40}... | collective-permute-start | bytes 786440 | tf_op jit(solution)/shard_map/ppermute | solution.py:191
  142.5 22.8 %collective-permute-start.27 = (bf16[2,64,1024]{2,1,0:T(8,128)(2,1)S(1)}, bf16[2,64,1024]{2,1,0:T(8,128)(2,1)S(1)}, u32[]{:S(2)}, u32[]{:S(2)}) collective-permute-start(bf16[2,64,1024]{2,1,0:T(8,128)(2,1)S(1)} %get-tuple-element.225), channel_id=1, source_target_pairs={{0,4},{4,8},{8,12},{16,20},{20,24},{24,28},{32,36},{36,40},{40,44}... | collective-permute-start | bytes 786440 | tf_op jit(solution)/shard_map/ppermute | solution.py:191
  153.8 21.1 %collective-permute-start.26 = (bf16[2,64,1024]{2,1,0:T(8,128)(2,1)S(1)}, bf16[2,64,1024]{2,1,0:T(8,128)(2,1)S(1)}, u32[]{:S(2)}, u32[]{:S(2)}) collective-permute-start(bf16[2,64,1024]{2,1,0:T(8,128)(2,1)S(1)} %get-tuple-element.224), channel_id=1, source_target_pairs={{0,4},{4,8},{8,12},{16,20},{20,24},{24,28},{32,36},{36,40},{40,44}... | collective-permute-start | bytes 786440 | tf_op jit(solution)/shard_map/ppermute | solution.py:191
  160.5 22.5 %collective-permute-start.7 = (bf16[2,64,1024]{2,1,0:T(8,128)(2,1)S(1)}, bf16[2,64,1024]{2,1,0:T(8,128)(2,1)S(1)}, u32[]{:S(2)}, u32[]{:S(2)}) collective-permute-start(bf16[2,64,1024]{2,1,0:T(8,128)(2,1)S(1)} %get-tuple-element.162), channel_id=1, source_target_pairs={{4,0},{8,4},{12,8},{20,16},{24,20},{28,24},{36,32},{40,36},{44,40}... | collective-permute-start | bytes 786440 | tf_op jit(solution)/shard_map/ppermute | solution.py:191
  163.9 22.5 %collective-permute-start.6 = (bf16[2,64,1024]{2,1,0:T(8,128)(2,1)S(1)}, bf16[2,64,1024]{2,1,0:T(8,128)(2,1)S(1)}, u32[]{:S(2)}, u32[]{:S(2)}) collective-permute-start(bf16[2,64,1024]{2,1,0:T(8,128)(2,1)S(1)} %get-tuple-element.161), channel_id=1, source_target_pairs={{4,0},{8,4},{12,8},{20,16},{24,20},{28,24},{36,32},{40,36},{44,40}... | collective-permute-start | bytes 786440 | tf_op jit(solution)/shard_map/ppermute | solution.py:191
  169.0 20.9 %collective-permute-start.29 = (bf16[2,64,1024]{2,1,0:T(8,128)(2,1)S(1)}, bf16[2,64,1024]{2,1,0:T(8,128)(2,1)S(1)}, u32[]{:S(2)}, u32[]{:S(2)}) collective-permute-start(bf16[2,64,1024]{2,1,0:T(8,128)(2,1)S(1)} %get-tuple-element.231), channel_id=1, source_target_pairs={{0,4},{4,8},{8,12},{16,20},{20,24},{24,28},{32,36},{36,40},{40,44}... | collective-permute-start | bytes 786440 | tf_op jit(solution)/shard_map/ppermute | solution.py:191
  178.4 21.1 %collective-permute-start.28 = (bf16[2,64,1024]{2,1,0:T(8,128)(2,1)S(1)}, bf16[2,64,1024]{2,1,0:T(8,128)(2,1)S(1)}, u32[]{:S(2)}, u32[]{:S(2)}) collective-permute-start(bf16[2,64,1024]{2,1,0:T(8,128)(2,1)S(1)} %get-tuple-element.230), channel_id=1, source_target_pairs={{0,4},{4,8},{8,12},{16,20},{20,24},{24,28},{32,36},{36,40},{40,44}... | collective-permute-start | bytes 786440 | tf_op jit(solution)/shard_map/ppermute | solution.py:191
  185.2 22.7 %collective-permute-start.9 = (bf16[2,64,1024]{2,1,0:T(8,128)(2,1)S(1)}, bf16[2,64,1024]{2,1,0:T(8,128)(2,1)S(1)}, u32[]{:S(2)}, u32[]{:S(2)}) collective-permute-start(bf16[2,64,1024]{2,1,0:T(8,128)(2,1)S(1)} %get-tuple-element.168), channel_id=1, source_target_pairs={{4,0},{8,4},{12,8},{20,16},{24,20},{28,24},{36,32},{40,36},{44,40}... | collective-permute-start | bytes 786440 | tf_op jit(solution)/shard_map/ppermute | solution.py:191
  188.5 22.7 %collective-permute-start.8 = (bf16[2,64,1024]{2,1,0:T(8,128)(2,1)S(1)}, bf16[2,64,1024]{2,1,0:T(8,128)(2,1)S(1)}, u32[]{:S(2)}, u32[]{:S(2)}) collective-permute-start(bf16[2,64,1024]{2,1,0:T(8,128)(2,1)S(1)} %get-tuple-element.167), channel_id=1, source_target_pairs={{4,0},{8,4},{12,8},{20,16},{24,20},{28,24},{36,32},{40,36},{44,40}... | collective-permute-start | bytes 786440 | tf_op jit(solution)/shard_map/ppermute | solution.py:191
  193.6 21.1 %collective-permute-start.31 = (bf16[2,64,1024]{2,1,0:T(8,128)(2,1)S(1)}, bf16[2,64,1024]{2,1,0:T(8,128)(2,1)S(1)}, u32[]{:S(2)}, u32[]{:S(2)}) collective-permute-start(bf16[2,64,1024]{2,1,0:T(8,128)(2,1)S(1)} %get-tuple-element.237), channel_id=1, source_target_pairs={{0,4},{4,8},{8,12},{16,20},{20,24},{24,28},{32,36},{36,40},{40,44}... | collective-permute-start | bytes 786440 | tf_op jit(solution)/shard_map/ppermute | solution.py:191
  203.0 21.2 %collective-permute-start.30 = (bf16[2,64,1024]{2,1,0:T(8,128)(2,1)S(1)}, bf16[2,64,1024]{2,1,0:T(8,128)(2,1)S(1)}, u32[]{:S(2)}, u32[]{:S(2)}) collective-permute-start(bf16[2,64,1024]{2,1,0:T(8,128)(2,1)S(1)} %get-tuple-element.236), channel_id=1, source_target_pairs={{0,4},{4,8},{8,12},{16,20},{20,24},{24,28},{32,36},{36,40},{40,44}... | collective-permute-start | bytes 786440 | tf_op jit(solution)/shard_map/ppermute | solution.py:191
  209.9 22.5 %collective-permute-start.11 = (bf16[2,64,1024]{2,1,0:T(8,128)(2,1)S(1)}, bf16[2,64,1024]{2,1,0:T(8,128)(2,1)S(1)}, u32[]{:S(2)}, u32[]{:S(2)}) collective-permute-start(bf16[2,64,1024]{2,1,0:T(8,128)(2,1)S(1)} %get-tuple-element.174), channel_id=1, source_target_pairs={{4,0},{8,4},{12,8},{20,16},{24,20},{28,24},{36,32},{40,36},{44,40}... | collective-permute-start | bytes 786440 | tf_op jit(solution)/shard_map/ppermute | solution.py:191
  213.3 22.5 %collective-permute-start.10 = (bf16[2,64,1024]{2,1,0:T(8,128)(2,1)S(1)}, bf16[2,64,1024]{2,1,0:T(8,128)(2,1)S(1)}, u32[]{:S(2)}, u32[]{:S(2)}) collective-permute-start(bf16[2,64,1024]{2,1,0:T(8,128)(2,1)S(1)} %get-tuple-element.173), channel_id=1, source_target_pairs={{4,0},{8,4},{12,8},{20,16},{24,20},{28,24},{36,32},{40,36},{44,40}... | collective-permute-start | bytes 786440 | tf_op jit(solution)/shard_map/ppermute | solution.py:191
  218.4 20.9 %collective-permute-start.33 = (bf16[2,64,1024]{2,1,0:T(8,128)(2,1)S(1)}, bf16[2,64,1024]{2,1,0:T(8,128)(2,1)S(1)}, u32[]{:S(2)}, u32[]{:S(2)}) collective-permute-start(bf16[2,64,1024]{2,1,0:T(8,128)(2,1)S(1)} %get-tuple-element.243), channel_id=1, source_target_pairs={{0,4},{4,8},{8,12},{16,20},{20,24},{24,28},{32,36},{36,40},{40,44}... | collective-permute-start | bytes 786440 | tf_op jit(solution)/shard_map/ppermute | solution.py:191
  227.8 21.1 %collective-permute-start.32 = (bf16[2,64,1024]{2,1,0:T(8,128)(2,1)S(1)}, bf16[2,64,1024]{2,1,0:T(8,128)(2,1)S(1)}, u32[]{:S(2)}, u32[]{:S(2)}) collective-permute-start(bf16[2,64,1024]{2,1,0:T(8,128)(2,1)S(1)} %get-tuple-element.242), channel_id=1, source_target_pairs={{0,4},{4,8},{8,12},{16,20},{20,24},{24,28},{32,36},{36,40},{40,44}... | collective-permute-start | bytes 786440 | tf_op jit(solution)/shard_map/ppermute | solution.py:191
  234.5 22.5 %collective-permute-start.13 = (bf16[2,64,1024]{2,1,0:T(8,128)(2,1)S(1)}, bf16[2,64,1024]{2,1,0:T(8,128)(2,1)S(1)}, u32[]{:S(2)}, u32[]{:S(2)}) collective-permute-start(bf16[2,64,1024]{2,1,0:T(8,128)(2,1)S(1)} %get-tuple-element.180), channel_id=1, source_target_pairs={{4,0},{8,4},{12,8},{20,16},{24,20},{28,24},{36,32},{40,36},{44,40}... | collective-permute-start | bytes 786440 | tf_op jit(solution)/shard_map/ppermute | solution.py:191
  237.9 22.7 %collective-permute-start.12 = (bf16[2,64,1024]{2,1,0:T(8,128)(2,1)S(1)}, bf16[2,64,1024]{2,1,0:T(8,128)(2,1)S(1)}, u32[]{:S(2)}, u32[]{:S(2)}) collective-permute-start(bf16[2,64,1024]{2,1,0:T(8,128)(2,1)S(1)} %get-tuple-element.179), channel_id=1, source_target_pairs={{4,0},{8,4},{12,8},{20,16},{24,20},{28,24},{36,32},{40,36},{44,40}... | collective-permute-start | bytes 786440 | tf_op jit(solution)/shard_map/ppermute | solution.py:191
  243.0 21.1 %collective-permute-start.35 = (bf16[2,64,1024]{2,1,0:T(8,128)(2,1)S(1)}, bf16[2,64,1024]{2,1,0:T(8,128)(2,1)S(1)}, u32[]{:S(2)}, u32[]{:S(2)}) collective-permute-start(bf16[2,64,1024]{2,1,0:T(8,128)(2,1)S(1)} %get-tuple-element.249), channel_id=1, source_target_pairs={{0,4},{4,8},{8,12},{16,20},{20,24},{24,28},{32,36},{36,40},{40,44}... | collective-permute-start | bytes 786440 | tf_op jit(solution)/shard_map/ppermute | solution.py:191
  252.4 21.3 %collective-permute-start.34 = (bf16[2,64,1024]{2,1,0:T(8,128)(2,1)S(1)}, bf16[2,64,1024]{2,1,0:T(8,128)(2,1)S(1)}, u32[]{:S(2)}, u32[]{:S(2)}) collective-permute-start(bf16[2,64,1024]{2,1,0:T(8,128)(2,1)S(1)} %get-tuple-element.248), channel_id=1, source_target_pairs={{0,4},{4,8},{8,12},{16,20},{20,24},{24,28},{32,36},{36,40},{40,44}... | collective-permute-start | bytes 786440 | tf_op jit(solution)/shard_map/ppermute | solution.py:191
  259.4 22.5 %collective-permute-start.15 = (bf16[2,64,1024]{2,1,0:T(8,128)(2,1)S(1)}, bf16[2,64,1024]{2,1,0:T(8,128)(2,1)S(1)}, u32[]{:S(2)}, u32[]{:S(2)}) collective-permute-start(bf16[2,64,1024]{2,1,0:T(8,128)(2,1)S(1)} %get-tuple-element.186), channel_id=1, source_target_pairs={{4,0},{8,4},{12,8},{20,16},{24,20},{28,24},{36,32},{40,36},{44,40}... | collective-permute-start | bytes 786440 | tf_op jit(solution)/shard_map/ppermute | solution.py:191
  262.8 29.9 %collective-permute-start.14 = (bf16[2,64,1024]{2,1,0:T(8,128)(2,1)S(1)}, bf16[2,64,1024]{2,1,0:T(8,128)(2,1)S(1)}, u32[]{:S(2)}, u32[]{:S(2)}) collective-permute-start(bf16[2,64,1024]{2,1,0:T(8,128)(2,1)S(1)} %get-tuple-element.185), channel_id=1, source_target_pairs={{4,0},{8,4},{12,8},{20,16},{24,20},{28,24},{36,32},{40,36},{44,40}... | collective-permute-start | bytes 786440 | tf_op jit(solution)/shard_map/ppermute | solution.py:191
  268.5 27.5 %collective-permute-start.37 = (bf16[2,64,1024]{2,1,0:T(8,128)(2,1)S(1)}, bf16[2,64,1024]{2,1,0:T(8,128)(2,1)S(1)}, u32[]{:S(2)}, u32[]{:S(2)}) collective-permute-start(bf16[2,64,1024]{2,1,0:T(8,128)(2,1)S(1)} %get-tuple-element.255), channel_id=1, source_target_pairs={{0,4},{4,8},{8,12},{16,20},{20,24},{24,28},{32,36},{36,40},{40,44}... | collective-permute-start | bytes 786440 | tf_op jit(solution)/shard_map/ppermute | solution.py:191
  278.0 33.9 %collective-permute-start.36 = (bf16[2,64,1024]{2,1,0:T(8,128)(2,1)S(1)}, bf16[2,64,1024]{2,1,0:T(8,128)(2,1)S(1)}, u32[]{:S(2)}, u32[]{:S(2)}) collective-permute-start(bf16[2,64,1024]{2,1,0:T(8,128)(2,1)S(1)} %get-tuple-element.254), channel_id=1, source_target_pairs={{0,4},{4,8},{8,12},{16,20},{20,24},{24,28},{32,36},{36,40},{40,44}... | collective-permute-start | bytes 786440 | tf_op jit(solution)/shard_map/ppermute | solution.py:191
  284.0 42.3 %collective-permute-start.17 = (bf16[2,64,1024]{2,1,0:T(8,128)(2,1)S(1)}, bf16[2,64,1024]{2,1,0:T(8,128)(2,1)S(1)}, u32[]{:S(2)}, u32[]{:S(2)}) collective-permute-start(bf16[2,64,1024]{2,1,0:T(8,128)(2,1)S(1)} %get-tuple-element.192), channel_id=1, source_target_pairs={{4,0},{8,4},{20,16},{24,20},{36,32},{40,36},{52,48},{56,52},{68,64... | collective-permute-start | bytes 786440 | tf_op jit(solution)/shard_map/ppermute | solution.py:191
  294.7 42.3 %collective-permute-start.16 = (bf16[2,64,1024]{2,1,0:T(8,128)(2,1)S(1)}, bf16[2,64,1024]{2,1,0:T(8,128)(2,1)S(1)}, u32[]{:S(2)}, u32[]{:S(2)}) collective-permute-start(bf16[2,64,1024]{2,1,0:T(8,128)(2,1)S(1)} %get-tuple-element.191), channel_id=1, source_target_pairs={{4,0},{8,4},{20,16},{24,20},{36,32},{40,36},{52,48},{56,52},{68,64... | collective-permute-start | bytes 786440 | tf_op jit(solution)/shard_map/ppermute | solution.py:191
  299.0 41.9 %collective-permute-start.39 = (bf16[2,64,1024]{2,1,0:T(8,128)(2,1)S(1)}, bf16[2,64,1024]{2,1,0:T(8,128)(2,1)S(1)}, u32[]{:S(2)}, u32[]{:S(2)}) collective-permute-start(bf16[2,64,1024]{2,1,0:T(8,128)(2,1)S(1)} %get-tuple-element.261), channel_id=1, source_target_pairs={{4,8},{8,12},{20,24},{24,28},{36,40},{40,44},{52,56},{56,60},{68,7... | collective-permute-start | bytes 786440 | tf_op jit(solution)/shard_map/ppermute | solution.py:191
  314.6 38.4 %collective-permute-start.38 = (bf16[2,64,1024]{2,1,0:T(8,128)(2,1)S(1)}, bf16[2,64,1024]{2,1,0:T(8,128)(2,1)S(1)}, u32[]{:S(2)}, u32[]{:S(2)}) collective-permute-start(bf16[2,64,1024]{2,1,0:T(8,128)(2,1)S(1)} %get-tuple-element.260), channel_id=1, source_target_pairs={{4,8},{8,12},{20,24},{24,28},{36,40},{40,44},{52,56},{56,60},{68,7... | collective-permute-start | bytes 786440 | tf_op jit(solution)/shard_map/ppermute | solution.py:191
  328.4 39.0 %collective-permute-start.19 = (bf16[2,64,1024]{2,1,0:T(8,128)(2,1)S(1)}, bf16[2,64,1024]{2,1,0:T(8,128)(2,1)S(1)}, u32[]{:S(2)}, u32[]{:S(2)}) collective-permute-start(bf16[2,64,1024]{2,1,0:T(8,128)(2,1)S(1)} %get-tuple-element.198), channel_id=1, source_target_pairs={{4,0},{20,16},{36,32},{52,48},{68,64},{84,80},{100,96},{116,112},{... | collective-permute-start | bytes 786440 | tf_op jit(solution)/shard_map/ppermute | solution.py:191
  339.6 30.7 %collective-permute-start.18 = (bf16[2,64,1024]{2,1,0:T(8,128)(2,1)S(1)}, bf16[2,64,1024]{2,1,0:T(8,128)(2,1)S(1)}, u32[]{:S(2)}, u32[]{:S(2)}) collective-permute-start(bf16[2,64,1024]{2,1,0:T(8,128)(2,1)S(1)} %get-tuple-element.197), channel_id=1, source_target_pairs={{4,0},{20,16},{36,32},{52,48},{68,64},{84,80},{100,96},{116,112},{... | collective-permute-start | bytes 786440 | tf_op jit(solution)/shard_map/ppermute | solution.py:191
  343.8 29.2 %collective-permute-start.41 = (bf16[2,64,1024]{2,1,0:T(8,128)(2,1)S(1)}, bf16[2,64,1024]{2,1,0:T(8,128)(2,1)S(1)}, u32[]{:S(2)}, u32[]{:S(2)}) collective-permute-start(bf16[2,64,1024]{2,1,0:T(8,128)(2,1)S(1)} %get-tuple-element.267), channel_id=1, source_target_pairs={{8,12},{24,28},{40,44},{56,60},{72,76},{88,92},{104,108},{120,124}... | collective-permute-start | bytes 786440 | tf_op jit(solution)/shard_map/ppermute | solution.py:191
  355.8 22.4 %collective-permute-start.40 = (bf16[2,64,1024]{2,1,0:T(8,128)(2,1)S(1)}, bf16[2,64,1024]{2,1,0:T(8,128)(2,1)S(1)}, u32[]{:S(2)}, u32[]{:S(2)}) collective-permute-start(bf16[2,64,1024]{2,1,0:T(8,128)(2,1)S(1)} %get-tuple-element.266), channel_id=1, source_target_pairs={{8,12},{24,28},{40,44},{56,60},{72,76},{88,92},{104,108},{120,124}... | collective-permute-start | bytes 786440 | tf_op jit(solution)/shard_map/ppermute | solution.py:191
  380.5 0.8 collective-permute-start.42
  382.2 0.8 collective-permute-start.43
  385.4 0.9 collective-permute-start.45
  395.1 3.6 collective-permute-start.51
  396.0 35.9 %collective-permute-start.52 = (bf16[2,128,1024]{2,1,0:T(8,128)(2,1)S(1)}, bf16[2,128,1024]{2,1,0:T(8,128)(2,1)S(1)}, u32[]{:S(2)}, u32[]{:S(2)}) collective-permute-start(bf16[2,128,1024]{2,1,0:T(8,128)(2,1)S(1)} %bitcast.433), channel_id=1, source_target_pairs={{12,16},{28,32},{44,48},{60,64},{76,80},{92,96},{108,112},{13,17},... | collective-permute-start | bytes 1572872 | tf_op jit(solution)/shard_map/ppermute | solution.py:243
  397.3 34.6 %collective-permute-start.53 = (bf16[2,128,1024]{2,1,0:T(8,128)(2,1)S(1)}, bf16[2,128,1024]{2,1,0:T(8,128)(2,1)S(1)}, u32[]{:S(2)}, u32[]{:S(2)}) collective-permute-start(bf16[2,128,1024]{2,1,0:T(8,128)(2,1)S(1)} %bitcast.434), channel_id=1, source_target_pairs={{12,20},{28,36},{44,52},{60,68},{76,84},{92,100},{108,116},{13,21}... | collective-permute-start | bytes 1572872 | tf_op jit(solution)/shard_map/ppermute | solution.py:243
  398.0 33.9 %collective-permute-start.54 = (bf16[2,128,1024]{2,1,0:T(8,128)(2,1)S(1)}, bf16[2,128,1024]{2,1,0:T(8,128)(2,1)S(1)}, u32[]{:S(2)}, u32[]{:S(2)}) collective-permute-start(bf16[2,128,1024]{2,1,0:T(8,128)(2,1)S(1)} %bitcast.435), channel_id=1, source_target_pairs={{12,24},{28,40},{44,56},{60,72},{76,88},{92,104},{108,120},{13,25}... | collective-permute-start | bytes 1572872 | tf_op jit(solution)/shard_map/ppermute | solution.py:243
  436.6 0.8 collective-permute-start.55
  439.0 0.8 collective-permute-start.56
  441.4 35.6 %collective-permute-start.57 = (bf16[2,32,1024]{2,1,0:T(8,128)(2,1)S(1)}, bf16[2,32,1024]{2,1,0:T(8,128)(2,1)S(1)}, u32[]{:S(2)}, u32[]{:S(2)}) collective-permute-start(bf16[2,32,1024]{2,1,0:T(8,128)(2,1)S(1)} %shard_map.96), channel_id=1, source_target_pairs={{4,0},{8,4},{12,8},{20,16},{24,20},{28,24},{36,32},{40,36},{44,40}... | collective-permute-start | bytes 393224 | tf_op jit(solution)/shard_map/ppermute | solution.py:287
  478.6 7.2 %collective-permute-start.58 = (bf16[2,32,1024]{2,1,0:T(8,128)(2,1)S(1)}, bf16[2,32,1024]{2,1,0:T(8,128)(2,1)S(1)}, u32[]{:S(2)}, u32[]{:S(2)}) collective-permute-start(bf16[2,32,1024]{2,1,0:T(8,128)(2,1)S(1)} %shard_map.97), channel_id=1, source_target_pairs={{4,0},{8,4},{12,8},{20,16},{24,20},{28,24},{36,32},{40,36},{44,40}... | collective-permute-start | bytes 393224 | tf_op jit(solution)/shard_map/ppermute | solution.py:287
  487.5 6.9 %collective-permute-start.59 = (bf16[2,32,1024]{2,1,0:T(8,128)(2,1)S(1)}, bf16[2,32,1024]{2,1,0:T(8,128)(2,1)S(1)}, u32[]{:S(2)}, u32[]{:S(2)}) collective-permute-start(bf16[2,32,1024]{2,1,0:T(8,128)(2,1)S(1)} %shard_map.98), channel_id=1, source_target_pairs={{4,0},{8,4},{20,16},{24,20},{36,32},{40,36},{52,48},{56,52},{68,64... | collective-permute-start | bytes 393224 | tf_op jit(solution)/shard_map/ppermute | solution.py:287
  495.9 6.9 %collective-permute-start.60 = (bf16[2,32,1024]{2,1,0:T(8,128)(2,1)S(1)}, bf16[2,32,1024]{2,1,0:T(8,128)(2,1)S(1)}, u32[]{:S(2)}, u32[]{:S(2)}) collective-permute-start(bf16[2,32,1024]{2,1,0:T(8,128)(2,1)S(1)} %shard_map.99), channel_id=1, source_target_pairs={{4,0},{20,16},{36,32},{52,48},{68,64},{84,80},{100,96},{116,112},{... | collective-permute-start | bytes 393224 | tf_op jit(solution)/shard_map/ppermute | solution.py:287
  507.1 0.8 collective-permute-start.62
  513.6 59.2 %collective-permute-start.66 = (bf16[2,32,1024]{2,1,0:T(8,128)(2,1)S(1)}, bf16[2,32,1024]{2,1,0:T(8,128)(2,1)S(1)}, u32[]{:S(2)}, u32[]{:S(2)}) collective-permute-start(bf16[2,32,1024]{2,1,0:T(8,128)(2,1)S(1)} %shard_map.106), channel_id=1, source_target_pairs={{32,16},{48,32},{64,48},{80,64},{33,17},{49,33},{65,49},{81,65},{3... | collective-permute-start | bytes 393224 | tf_op jit(solution)/shard_map/ppermute | solution.py:301
  573.6 7.8 %collective-permute-start.67 = (bf16[2,32,1024]{2,1,0:T(8,128)(2,1)S(1)}, bf16[2,32,1024]{2,1,0:T(8,128)(2,1)S(1)}, u32[]{:S(2)}, u32[]{:S(2)}) collective-permute-start(bf16[2,32,1024]{2,1,0:T(8,128)(2,1)S(1)} %shard_map.107), channel_id=1, source_target_pairs={{16,0},{32,16},{48,32},{64,48},{17,1},{33,17},{49,33},{65,49},{18,... | collective-permute-start | bytes 393224 | tf_op jit(solution)/shard_map/ppermute | solution.py:301
  582.2 7.8 %collective-permute-start.68 = (bf16[2,32,1024]{2,1,0:T(8,128)(2,1)S(1)}, bf16[2,32,1024]{2,1,0:T(8,128)(2,1)S(1)}, u32[]{:S(2)}, u32[]{:S(2)}) collective-permute-start(bf16[2,32,1024]{2,1,0:T(8,128)(2,1)S(1)} %shard_map.108), channel_id=1, source_target_pairs={{16,0},{32,16},{48,32},{17,1},{33,17},{49,33},{18,2},{34,18},{50,3... | collective-permute-start | bytes 393224 | tf_op jit(solution)/shard_map/ppermute | solution.py:301
  590.8 7.8 %collective-permute-start.69 = (bf16[2,32,1024]{2,1,0:T(8,128)(2,1)S(1)}, bf16[2,32,1024]{2,1,0:T(8,128)(2,1)S(1)}, u32[]{:S(2)}, u32[]{:S(2)}) collective-permute-start(bf16[2,32,1024]{2,1,0:T(8,128)(2,1)S(1)} %shard_map.109), channel_id=1, source_target_pairs={{16,0},{32,16},{17,1},{33,17},{18,2},{34,18},{19,3},{35,19}} | collective-permute-start | bytes 393224 | tf_op jit(solution)/shard_map/ppermute | solution.py:301
  599.4 5.5 collective-permute-start.70
  600.9 8.0 %collective-permute-start.71 = (bf16[2,128,1024]{2,1,0:T(8,128)(2,1)S(1)}, bf16[2,128,1024]{2,1,0:T(8,128)(2,1)S(1)}, u32[]{:S(2)}, u32[]{:S(2)}) collective-permute-start(bf16[2,128,1024]{2,1,0:T(8,128)(2,1)S(1)} %bitcast.436), channel_id=1, source_target_pairs={{16,4},{32,20},{48,36},{64,52},{80,68},{96,84},{112,100},{17,5},{3... | collective-permute-start | bytes 1572872 | tf_op jit(solution)/shard_map/ppermute | solution.py:306
  602.3 12.3 %collective-permute-start.72 = (bf16[2,128,1024]{2,1,0:T(8,128)(2,1)S(1)}, bf16[2,128,1024]{2,1,0:T(8,128)(2,1)S(1)}, u32[]{:S(2)}, u32[]{:S(2)}) collective-permute-start(bf16[2,128,1024]{2,1,0:T(8,128)(2,1)S(1)} %bitcast.437), channel_id=1, source_target_pairs={{16,8},{32,24},{48,40},{64,56},{80,72},{96,88},{112,104},{17,9},{3... | collective-permute-start | bytes 1572872 | tf_op jit(solution)/shard_map/ppermute | solution.py:306
  603.6 10.9 %collective-permute-start.73 = (bf16[2,128,1024]{2,1,0:T(8,128)(2,1)S(1)}, bf16[2,128,1024]{2,1,0:T(8,128)(2,1)S(1)}, u32[]{:S(2)}, u32[]{:S(2)}) collective-permute-start(bf16[2,128,1024]{2,1,0:T(8,128)(2,1)S(1)} %bitcast.438), channel_id=1, source_target_pairs={{16,12},{32,28},{48,44},{64,60},{80,76},{96,92},{112,108},{17,13},... | collective-permute-start | bytes 1572872 | tf_op jit(solution)/shard_map/ppermute | solution.py:306
  (56 other events, 272.4 us)

commit v2 on v0

v2 whole, which is shorter than its diff:
```python
import functools

import jax
import jax.numpy as jnp
from jax import lax
from jax.experimental import pallas as pl
from jax.experimental.pallas import tpu as pltpu
from jax.sharding import PartitionSpec as P

GROUP = 4
BATCHES = 4
LAG = 2
AXIS = "strip"
BF16 = jnp.bfloat16
F32 = jnp.float32
MIB = 2**20

VMEM = pl.BlockSpec(memory_space=pltpu.VMEM)
SMEM = pl.BlockSpec(memory_space=pltpu.SMEM)
ANY = pl.BlockSpec(memory_space=pl.ANY)
PLAIN = (((1,), (0,)), ((), ()))
TURNED = (((1,), (1,)), ((), ()))


def resident(value):
    return pltpu.with_memory_space_constraint(value, pltpu.VMEM)


def held(*shape, dtype=BF16):
    return pltpu.VMEM(shape, dtype)


def whole(value):
    return jax.ShapeDtypeStruct(value.shape, value.dtype)


def call(kernel, outs, operands, specs, scratch=(), aliases=None, rows=32, times=1, limit=12):
    size = 1024
    return pl.pallas_call(
        kernel,
        out_shape=outs,
        in_specs=specs,
        out_specs=jax.tree.map(lambda _: VMEM, outs),
        scratch_shapes=scratch,
        input_output_aliases=aliases or {},
        compiler_params=pltpu.CompilerParams(vmem_limit_bytes=limit * MIB),
        cost_estimate=pl.CostEstimate(
            flops=8 * times * rows * size * size, bytes_accessed=4 * times * size * size, transcendentals=0
        ),
    )(*operands)


def product(direct, crossed, real, imag, out, tile, turned):
    dims = TURNED if turned else PLAIN
    tile = min(tile, real.shape[0])

    def body(step, carry):
        columns = pl.ds(pl.multiple_of(step * tile, tile), tile)
        where = (columns, slice(None)) if turned else (slice(None), columns)
        out(
            columns,
            lax.dot_general(direct[...], real[where], dims, preferred_element_type=F32)
            + lax.dot_general(crossed[...], imag[where], dims, preferred_element_type=F32),
        )
        return carry

    lax.fori_loop(0, real.shape[0] // tile, body, 0)


def spread(rows, direct, crossed):
    count = direct.shape[0] // 2
    direct[:count] = rows[0]
    direct[count:] = rows[1]
    crossed[:count] = -rows[1]
    crossed[count:] = rows[0]


def halves(value):
    return value.reshape(2, value.shape[0] // 2, value.shape[1])


def stage_kernel(real, imag, real_out, imag_out, sems):
    copies = [
        pltpu.make_async_copy(real, real_out, sems.at[0]),
        pltpu.make_async_copy(imag, imag_out, sems.at[1]),
    ]
    for copy in copies:
        copy.start()
    for copy in copies:
        copy.wait()


def between(index, count):
    return jnp.logical_and(index >= 0, index < count)


def sweep_kernel(step, aliased, place_ref, block_f, block_b, real, imag, source, *refs):
    own_f, got_f, own_b, got_b, out_f, out_b, direct, crossed, result = refs[4:] if aliased else refs
    chunk, size = block_f.shape[1:]
    chunks = size // chunk
    place = place_ref[0]
    index_f = step - LAG * (place - 1)
    index_b = step - LAG * (GROUP - 2 - place)
    last = index_f == chunks
    active_f, active_b = between(index_f, chunks + 1), between(index_b, chunks)
    row_f, row_b = (jnp.clip(index, 0, chunks) * chunk for index in (index_f, index_b))

    for way, (block, row, active, starts) in enumerate(
        (
            (block_f, row_f, active_f, jnp.logical_and(place == 0, jnp.logical_not(last))),
            (block_b, row_b, active_b, place == GROUP - 1),
        )
    ):

        @pl.when(jnp.logical_and(active, starts))
        def _(way=way, row=row):
            shape = (chunk, size)
            hit = lax.broadcasted_iota(jnp.int32, shape, 1) == lax.broadcasted_iota(jnp.int32, shape, 0) + row
            one = jnp.where(hit, 1.0, 0.0).astype(BF16)
            spread((one, jnp.zeros(shape, BF16)), direct.at[way], crossed.at[way])

        @pl.when(jnp.logical_and(active, jnp.logical_not(starts)))
        def _(way=way, block=block):
            spread(block, direct.at[way], crossed.at[way])

    @pl.when(last)
    def _():
        entered = (block_f[...].astype(F32) + source[0].astype(F32)).astype(BF16)
        spread(entered, direct.at[0], crossed.at[0])

    def multiply(way, layer):
        def keep(columns, value):
            result[way, :, :, columns] = halves(value)

        product(
            direct.at[way], crossed.at[way], real.at[layer], imag.at[layer], keep, 256, True
        )

    def both(way, carry):
        @pl.when(jnp.logical_or(jnp.logical_and(way == 0, active_f), jnp.logical_and(way == 1, active_b)))
        def _():
            multiply(way, way)

            @pl.when(jnp.logical_and(way == 0, last))
            def _():
                result[way] += source[1].astype(F32)

            spread(result[way].astype(BF16), direct.at[way], crossed.at[way])
            multiply(way, 1 - way)

        return carry

    lax.fori_loop(0, 2, both, 0)
    for way, (block, own, got, out, row, active) in enumerate(
        (
            (block_f, own_f, got_f, out_f, row_f, active_f),
            (block_b, own_b, got_b, out_b, row_b, active_b),
        )
    ):

        @pl.when(active)
        def _(way=way, row=row, block=block, own=own, got=got, out=out):
            rows = pl.ds(pl.multiple_of(row, chunk), chunk)
            done = result[way].astype(BF16)
            out[...] = done
            own[:, rows, :] = done
            got[:, rows, :] = block[...]


def sweep(step, place, block_f, block_b, real, imag, source, kept):
    _, chunk, size = block_f.shape
    outs = [whole(value) for value in kept] or [
        held(2, length, size) for length in (size + chunk,) * 2 + (size,) * 2
    ]
    return call(
        functools.partial(sweep_kernel, step, bool(kept)),
        (*outs, whole(block_f), whole(block_b)),
        (place, block_f, block_b, resident(real), resident(imag), resident(source), *map(resident, kept)),
        [SMEM] + [VMEM] * (5 + len(kept)),
        scratch=[
            pltpu.VMEM((2, 2 * chunk, size), BF16),
            pltpu.VMEM((2, 2 * chunk, size), BF16),
            pltpu.VMEM((2, 2, chunk, size), F32),
        ],
        aliases={6 + i: i for i in range(4)} if kept else None,
        rows=chunk,
        times=4,
    )


def stacked(count, size):
    return [pltpu.VMEM((2 * count, size), BF16)] * 2


def chain_kernel(moment, spread_from, inward, aliased, place_ref, block, matrix, constants, *refs):
    refs = refs[2:] if aliased else refs
    sent, came, out, copy, direct, crossed = refs
    size = block.shape[2]
    width = block.shape[1]
    place, group, far = place_ref[0], place_ref[1], place_ref[2]
    batch = moment - (far if inward else group)
    node = jnp.logical_and(place == (0 if inward else GROUP - 1), between(batch, BATCHES))
    sends = jnp.logical_and(node, (group if inward else far) > 0)
    index = jnp.clip(batch, 0, BATCHES - 1)

    @pl.when(node)
    def _():
        came[index] = block[...]

    @pl.when(sends)
    def _():
        spread(block, direct, crossed)

        def keep(columns, value):
            if inward:
                constant = constants[index, :, :, columns]
            else:
                constant = matrix[:, pl.ds(pl.multiple_of(size + index * width, width), width), columns]
            out[:, :, columns] = (halves(value) + constant.astype(F32)).astype(BF16)

        product(direct, crossed, matrix.at[0, :size], matrix.at[1, :size], keep, 512, False)
        sent[index] = out[...]

    if 0 <= moment - spread_from < BATCHES:
        copy[...] = sent[moment - spread_from]


def chain(moment, spread_from, inward, place, block, matrix, constants, kept):
    outs = [whole(value) for value in kept] or [held(BATCHES, *block.shape)] * 2
    *kept, out, copy = call(
        functools.partial(chain_kernel, moment, spread_from, inward, bool(kept)),
        (*outs, whole(block), whole(block)),
        (place, block, resident(matrix), resident(constants), *map(resident, kept)),
        [SMEM] + [VMEM] * (3 + len(kept)),
        scratch=stacked(*block.shape[1:]),
        aliases={4: 0, 5: 1} if kept else None,
    )
    return kept, out, copy


def pick_entry(place, mine, entries, came, batch, direct, crossed):
    @pl.when(place == mine)
    def _():
        spread(came.at[batch], direct, crossed)

    others = [other for other in range(GROUP) if other != mine]
    for other, entry in zip(others, entries):

        @pl.when(place == other)
        def _(entry=entry):
            spread(entry, direct, crossed)


def trace_kernel(batch, aliased, place_ref, *refs):
    *entries, came, before, source, real, imag = refs[: GROUP + 4]
    refs = refs[GROUP + 4 :]
    trace_first, trace_second, enter, direct, crossed = refs[2:] if aliased else refs
    size, width = before.shape[2], enter.shape[1]
    place = place_ref[0]
    rows = pl.ds(batch * width, width)
    pick_entry(place, GROUP - 1, entries, came, batch, direct, crossed)

    @pl.when(place == 0)
    def _():
        enter[...] = entries[0][...].astype(F32)

    @pl.when(place != 0)
    def _():
        def keep(columns, value):
            constant = before[:, pl.ds(size + batch * width, width), columns]
            enter[:, :, columns] = halves(value) + constant.astype(F32)

        product(direct, crossed, before.at[0, :size], before.at[1, :size], keep, 512, False)

    def keep_first(columns, value):
        trace_first[batch, :, :, columns] = halves(value)

    def keep_second(columns, value):
        trace_second[batch, :, :, columns] = halves(value)

    spread((source[0, :, rows, :].astype(F32) + enter[...]).astype(BF16), direct, crossed)
    product(direct, crossed, real.at[0], imag.at[0], keep_first, 512, True)
    spread((source[1, :, rows, :].astype(F32) + trace_first[batch]).astype(BF16), direct, crossed)
    product(direct, crossed, real.at[1], imag.at[1], keep_second, 512, True)


def inner_kernel(moment, aliased, place_ref, block, real, imag, trace_first, trace_second, *refs):
    sent, came, out, middle, direct, crossed = refs[2:] if aliased else refs
    mirror = GROUP - 1 - place_ref[0]
    batch = moment - mirror
    index = jnp.clip(batch, 0, BATCHES - 1)

    @pl.when(between(batch, BATCHES))
    def _():
        middle[...] = trace_second[index].astype(BF16)

        @pl.when(mirror != 0)
        def _():
            came[index] = block[...]
            spread(block, direct, crossed)

            def keep(columns, value):
                middle[:, :, columns] = (trace_second[index, :, :, columns] + halves(value)).astype(BF16)

            product(direct, crossed, real.at[1], imag.at[1], keep, 512, True)

        def keep_out(columns, value):
            out[:, :, columns] = (trace_first[index, :, :, columns] + halves(value)).astype(BF16)

        spread(middle, direct, crossed)
        product(direct, crossed, real.at[0], imag.at[0], keep_out, 512, True)
        sent[index] = out[...]


def field_kernel(batch, aliased, place_ref, *refs):
    *entries, came, after, constants, real, imag, trace_first, trace_second = refs[: GROUP + 6]
    refs = refs[GROUP + 6 :]
    out, enter, direct, crossed = refs[1:] if aliased else refs
    width = enter.shape[1]
    place = place_ref[0]
    rows = pl.ds(batch * width, width)
    pick_entry(place, 0, entries, came, batch, direct, crossed)

    @pl.when(place != GROUP - 1)
    def _():
        def keep(columns, value):
            enter[:, :, columns] = (halves(value) + constants[batch, :, :, columns].astype(F32)).astype(BF16)

        product(direct, crossed, after.at[0], after.at[1], keep, 512, False)
        spread(enter, direct, crossed)

    def keep_second(columns, value):
        enter[:, :, columns] = (trace_second[batch, :, :, columns] + halves(value)).astype(BF16)

    def keep_first(columns, value):
        out[0, :, rows, columns] = (trace_first[batch, :, :, columns] + halves(value)).astype(BF16)

    product(direct, crossed, real.at[1], imag.at[1], keep_second, 512, True)
    out[1, :, rows, :] = enter[...]
    spread(enter, direct, crossed)
    product(direct, crossed, real.at[0], imag.at[0], keep_first, 512, True)


def shards(source, pivot_inverse_real, factor_imag):
    strips = lax.axis_size(AXIS)
    groups = strips // GROUP
    position = lax.axis_index(AXIS)
    group = position // GROUP
    place = jnp.stack([position % GROUP, group, groups - 1 - group]).astype(jnp.int32)
    size = source.shape[1]
    columns = source.shape[3]
    width = columns // BATCHES
    chunk = columns
    chunks = size // chunk
    total = chunks + 1

    vectors = source.transpose(0, 2, 3, 1)
    real, imag = call(
        stage_kernel,
        tuple(held(*value.shape) for value in (pivot_inverse_real, factor_imag)),
        (pivot_inverse_real, factor_imag),
        [ANY, ANY],
        scratch=[pltpu.SemaphoreType.DMA((2,))],
    )

    nothing = jnp.zeros((2, chunk, size), BF16)
    up = [(s, s + 1) for s in range(strips) if s % GROUP != GROUP - 1]
    down = [(s + 1, s) for s, _ in up]

    def moved(outs, step, pairs, count):
        live = [
            (s, d)
            for s, d in pairs
            if 0 <= step - LAG * (s % GROUP if d > s else GROUP - 1 - s % GROUP) < count
        ]
        return lax.ppermute(outs[step - LAG], AXIS, live) if live and step >= 0 else nothing

    outs_f, outs_b = {}, {}
    kept = ()
    for step in range(-LAG, total + LAG * (GROUP - 2)):
        *kept, outs_f[step], outs_b[step] = sweep(
            step,
            place,
            moved(outs_f, step, up, total),
            moved(outs_b, step, down, chunks),
            real,
            imag,
            vectors,
            kept,
        )
    prefix, prefix_before, suffix, suffix_after = kept

    block = jax.ShapeDtypeStruct((2, width, size), BF16)
    nought = jnp.zeros((2, width, size), BF16)
    block_f = block_i = block_b = nought
    kept_f = kept_i = kept_b = traces = fields = ()
    spread_f, spread_b = {}, {}
    turn = groups - 2
    inner_start = turn + 1
    back_start = inner_start + GROUP - 1
    back_end = back_start + turn
    for moment in range(back_end + BATCHES + 1):
        if moment <= turn + BATCHES:
            kept_f, outgoing, copy = chain(
                moment, turn, False, place, block_f, prefix, vectors, kept_f
            )
            pairs = [
                (GROUP * g + GROUP - 1, GROUP * g + 2 * GROUP - 1)
                for g in range(groups - 1)
                if 0 <= moment - g < BATCHES
            ]
            if pairs:
                block_f = lax.ppermute(outgoing, AXIS, pairs)
            if 0 <= moment - turn < BATCHES:
                spread_f[moment - turn] = [
                    lax.ppermute(
                        copy,
                        AXIS,
                        [(GROUP * g + GROUP - 1, GROUP * g + GROUP + other) for g in range(groups - 1)],
                    )
                    for other in range(GROUP - 1)
                ]
        batch = moment - inner_start
        if 0 <= batch < BATCHES:
            outs = [whole(value) for value in traces] or [held(BATCHES, 2, width, size, dtype=F32)] * 2
            traces = call(
                functools.partial(trace_kernel, batch, bool(traces)),
                tuple(outs),
                (
                    place,
                    *spread_f[batch],
                    *map(resident, (kept_f[1], prefix_before, vectors, real, imag, *traces)),
                ),
                [SMEM] + [VMEM] * (GROUP + 4 + len(traces)),
                scratch=[pltpu.VMEM((2, width, size), F32)] + stacked(width, size),
                aliases={GROUP + 5: 0, GROUP + 6: 1} if traces else None,
                times=3,
            )
        if inner_start <= moment < back_start + BATCHES:
            outs = [whole(value) for value in kept_i] or [held(BATCHES, 2, width, size)] * 2
            *kept_i, outgoing = call(
                functools.partial(inner_kernel, moment - inner_start, bool(kept_i)),
                (*outs, block),
                (place, block_i, *map(resident, (real, imag, *traces, *kept_i))),
                [SMEM] + [VMEM] * (5 + len(kept_i)),
                scratch=[pltpu.VMEM((2, width, size), BF16)] + stacked(width, size),
                aliases={6: 0, 7: 1} if kept_i else None,
                times=2,
            )
            pairs = [
                (s, d)
                for s, d in down
                if 0 <= moment - inner_start - (GROUP - 1 - s % GROUP) < BATCHES
            ]
            if pairs:
                block_i = lax.ppermute(outgoing, AXIS, pairs)
        if back_start <= moment <= back_end + BATCHES:
            kept_b, outgoing, copy = chain(
                moment - back_start, turn, True, place, block_b, suffix, kept_i[0], kept_b
            )
            pairs = [
                (GROUP * g + GROUP, GROUP * g)
                for g in range(groups - 1)
                if 0 <= moment - back_start - (groups - 2 - g) < BATCHES
            ]
            if pairs:
                block_b = lax.ppermute(outgoing, AXIS, pairs)
            if 0 <= moment - back_end < BATCHES:
                spread_b[moment - back_end] = [
                    lax.ppermute(
                        copy,
                        AXIS,
                        [(GROUP * g + GROUP, GROUP * g + other) for g in range(groups - 1)],
                    )
                    for other in range(1, GROUP)
                ]
        batch = moment - back_end - 1
        if batch >= 0:
            fields = (
                call(
                    functools.partial(field_kernel, batch, bool(fields)),
                    whole(fields[0]) if fields else held(2, 2, columns, size),
                    (
                        place,
                        *spread_b[batch],
                        *map(
                            resident,
                            (kept_b[1], suffix_after, kept_i[1], real, imag, *traces, *fields),
                        ),
                    ),
                    [SMEM] + [VMEM] * (GROUP + 6 + len(fields)),
                    scratch=[pltpu.VMEM((2, width, size), BF16)] + stacked(width, size),
                    aliases={GROUP + 7: 0} if fields else None,
                    times=3,
                ),
            )
    return fields[0].transpose(0, 3, 1, 2)


def solution(mesh):
    placed = (P("strip", None, None, "wave"), P("strip", "wave", None), P("strip", "wave", None))
    return jax.shard_map(
        shards,
        mesh=mesh,
        in_specs=placed,
        out_specs=P("strip", None, None, "wave"),
        check_vma=False,
    )
```

time: 1240 us -> 536 us (0.43)
  waiting for transfers between devices: 794 us -> 43.6 us
  Pallas kernels: 0 us -> 158 us
  matrix products: 75.2 us -> 0 us
  starting transfers between devices: 338 us -> 315 us
    ppermute x70 -> x75, waiting for transfers between devices: 794 us -> 43.6 us  [the longest x6 18.8 us: shards(): block_i = lax.ppermute(outgoing, AXIS, pairs)]
    pallas_call x0 -> x53, Pallas kernels: none -> 158 us  [call(): pl.pallas_call(kernel, out_shape=outs, in_specs=specs, out_specs=jax.tree...]
    dot_general x32 -> x0, matrix products: 75.2 us -> none  [the longest x16 37.6 us: complex_apply(): jnp.dot(imag_part, merged, preferred_element_type=jnp.float32)]
    ppermute x70 -> x75, starting transfers between devices: 338 us -> 315 us  [the longest x25 169 us: moved(): lax.ppermute(outs[step - LAG], AXIS, live)]
  transfers between devices with their start and end apart: 70 -> 75, of which waited for: 70 -> 9; matrix products, arithmetic and copies ran while one was open for 0% -> 0% of each run, Pallas kernels for 0% -> 25%
where the time goes in v2:
time: 536 us; the launch traced here: 527 us
  starting transfers between devices  315 us (59%)
  Pallas kernels  158 us (29%)
  waiting for transfers between devices  43.6 us (8%)
  local copies, waits for them, and re-layouts  8.88 us (2%)
    ppermute x25, starting transfers between devices, moved(): lax.ppermute(outs[step - LAG], AXIS, live)  169 us
    pallas_call x53, Pallas kernels, call(): pl.pallas_call(kernel, out_shape=outs, in_specs=specs, out_specs=jax.tree...  158 us
    ppermute x10, starting transfers between devices, shards(): block_f = lax.ppermute(outgoing, AXIS, pairs)  78.3 us
    ppermute x10, starting transfers between devices, shards(): block_b = lax.ppermute(outgoing, AXIS, pairs)  34.9 us
    ppermute x6, waiting for transfers between devices, shards(): block_i = lax.ppermute(outgoing, AXIS, pairs)  18.8 us
    ppermute x12, starting transfers between devices, shards(): lax.ppermute(copy, AXIS, [(GROUP * g + GROUP, GROUP * g + other) for g in...  15.8 us
    ppermute x10, waiting for transfers between devices, shards(): block_b = lax.ppermute(outgoing, AXIS, pairs)  14.2 us
  transfers between devices with their start and end apart: 75, of which 9 were waited for; matrix products, arithmetic and copies ran while one was open for 0% of the time, Pallas kernels for 25%

profile of v2, /device:TPU:8, one launch (start us, length us, event | category | flops | bytes accessed | tf_op | source)
XLA Modules:
  0.0 527.2 jit_solution(17956946714096512059)
XLA Ops:
  0.0 2.4 copy.121
  2.5 2.2 copy-done
  4.7 2.2 copy-done.1
  7.6 4.6 shard_map.38
  12.2 10.6 %collective-permute-start = (bf16[2,128,1024]{2,1,0:T(8,128)(2,1)S(1)}, bf16[2,128,1024]{2,1,0:T(8,128)(2,1)S(1)}, u32[]{:S(2)}, u32[]{:S(2)}) collective-permute-start(bf16[2,128,1024]{2,1,0:T(8,128)(2,1)S(1)} %get-tuple-element.192), channel_id=1, source_target_pairs={{0,4},{16,20},{32,36},{48,52},{64,68},{80,84},{96,100},{112,116},{... | collective-permute-start | bytes 1572872 | tf_op jit(solution)/shard_map/ppermute | solution.py:376
  23.5 4.6 shard_map.39
  28.2 11.4 %collective-permute-start.4 = (bf16[2,128,1024]{2,1,0:T(8,128)(2,1)S(1)}, bf16[2,128,1024]{2,1,0:T(8,128)(2,1)S(1)}, u32[]{:S(2)}, u32[]{:S(2)}) collective-permute-start(bf16[2,128,1024]{2,1,0:T(8,128)(2,1)S(1)} %get-tuple-element.204), channel_id=1, source_target_pairs={{0,4},{16,20},{32,36},{48,52},{64,68},{80,84},{96,100},{112,116},{... | collective-permute-start | bytes 1572872 | tf_op jit(solution)/shard_map/ppermute | solution.py:376
  39.6 8.9 %collective-permute-start.5 = (bf16[2,128,1024]{2,1,0:T(8,128)(2,1)S(1)}, bf16[2,128,1024]{2,1,0:T(8,128)(2,1)S(1)}, u32[]{:S(2)}, u32[]{:S(2)}) collective-permute-start(bf16[2,128,1024]{2,1,0:T(8,128)(2,1)S(1)} %get-tuple-element.205), channel_id=1, source_target_pairs={{12,8},{28,24},{44,40},{60,56},{76,72},{92,88},{108,104},{124,120}... | collective-permute-start | bytes 1572872 | tf_op jit(solution)/shard_map/ppermute | solution.py:376
  48.5 4.6 shard_map.40
  53.1 10.6 %collective-permute-start.2 = (bf16[2,128,1024]{2,1,0:T(8,128)(2,1)S(1)}, bf16[2,128,1024]{2,1,0:T(8,128)(2,1)S(1)}, u32[]{:S(2)}, u32[]{:S(2)}) collective-permute-start(bf16[2,128,1024]{2,1,0:T(8,128)(2,1)S(1)} %get-tuple-element.202), channel_id=1, source_target_pairs={{0,4},{4,8},{16,20},{20,24},{32,36},{36,40},{48,52},{52,56},{64,68... | collective-permute-start | bytes 1572872 | tf_op jit(solution)/shard_map/ppermute | solution.py:376
  64.4 4.6 shard_map.41
  69.1 11.9 %collective-permute-start.8 = (bf16[2,128,1024]{2,1,0:T(8,128)(2,1)S(1)}, bf16[2,128,1024]{2,1,0:T(8,128)(2,1)S(1)}, u32[]{:S(2)}, u32[]{:S(2)}) collective-permute-start(bf16[2,128,1024]{2,1,0:T(8,128)(2,1)S(1)} %get-tuple-element.216), channel_id=1, source_target_pairs={{0,4},{4,8},{16,20},{20,24},{32,36},{36,40},{48,52},{52,56},{64,68... | collective-permute-start | bytes 1572872 | tf_op jit(solution)/shard_map/ppermute | solution.py:376
  81.0 8.9 %collective-permute-start.9 = (bf16[2,128,1024]{2,1,0:T(8,128)(2,1)S(1)}, bf16[2,128,1024]{2,1,0:T(8,128)(2,1)S(1)}, u32[]{:S(2)}, u32[]{:S(2)}) collective-permute-start(bf16[2,128,1024]{2,1,0:T(8,128)(2,1)S(1)} %get-tuple-element.217), channel_id=1, source_target_pairs={{8,4},{12,8},{24,20},{28,24},{40,36},{44,40},{56,52},{60,56},{72,6... | collective-permute-start | bytes 1572872 | tf_op jit(solution)/shard_map/ppermute | solution.py:376
  89.9 4.6 shard_map.42
  94.6 7.4 %collective-permute-start.6 = (bf16[2,128,1024]{2,1,0:T(8,128)(2,1)S(1)}, bf16[2,128,1024]{2,1,0:T(8,128)(2,1)S(1)}, u32[]{:S(2)}, u32[]{:S(2)}) collective-permute-start(bf16[2,128,1024]{2,1,0:T(8,128)(2,1)S(1)} %get-tuple-element.214), channel_id=1, source_target_pairs={{0,4},{4,8},{8,12},{16,20},{20,24},{24,28},{32,36},{36,40},{40,44}... | collective-permute-start | bytes 1572872 | tf_op jit(solution)/shard_map/ppermute | solution.py:376
  103.2 4.6 shard_map.43
  107.9 8.7 %collective-permute-start.12 = (bf16[2,128,1024]{2,1,0:T(8,128)(2,1)S(1)}, bf16[2,128,1024]{2,1,0:T(8,128)(2,1)S(1)}, u32[]{:S(2)}, u32[]{:S(2)}) collective-permute-start(bf16[2,128,1024]{2,1,0:T(8,128)(2,1)S(1)} %get-tuple-element.228), channel_id=1, source_target_pairs={{0,4},{4,8},{8,12},{16,20},{20,24},{24,28},{32,36},{36,40},{40,44}... | collective-permute-start | bytes 1572872 | tf_op jit(solution)/shard_map/ppermute | solution.py:376
  117.9 9.1 %shard_map.44 = (bf16[2,1152,1024]{2,1,0:T(8,128)(2,1)S(1)}, bf16[2,1152,1024]{2,1,0:T(8,128)(2,1)S(1)}, bf16[2,1024,1024]{2,1,0:T(8,128)(2,1)S(1)}, bf16[2,1024...) custom-call(s32[3]{0:T(128)S(1)} %pad_add_fusion.place_ref, ...), custom_call_target="tpu_custom_call", output_to_operand_aliasing={{0}: (6, {}), {1}: (7, {}), {2}: (8, {}), {3}: (9, {})} | custom-call | flops 4294967296 | bytes 16777216 | tf_op jit(solution)/shard_map/pallas_call | solution.py:39
  127.0 4.6 collective-permute-start.10
  132.9 8.6 %shard_map.45 = (bf16[2,1152,1024]{2,1,0:T(8,128)(2,1)S(1)}, bf16[2,1152,1024]{2,1,0:T(8,128)(2,1)S(1)}, bf16[2,1024,1024]{2,1,0:T(8,128)(2,1)S(1)}, bf16[2,1024...) custom-call(s32[3]{0:T(128)S(1)} %pad_add_fusion.place_ref, ...), custom_call_target="tpu_custom_call", output_to_operand_aliasing={{0}: (6, {}), {1}: (7, {}), {2}: (8, {}), {3}: (9, {})} | custom-call | flops 4294967296 | bytes 16777216 | tf_op jit(solution)/shard_map/pallas_call | solution.py:39
  141.5 4.6 collective-permute-start.16
  147.4 8.9 %shard_map.46 = (bf16[2,1152,1024]{2,1,0:T(8,128)(2,1)S(1)}, bf16[2,1152,1024]{2,1,0:T(8,128)(2,1)S(1)}, bf16[2,1024,1024]{2,1,0:T(8,128)(2,1)S(1)}, bf16[2,1024...) custom-call(s32[3]{0:T(128)S(1)} %pad_add_fusion.place_ref, ...), custom_call_target="tpu_custom_call", output_to_operand_aliasing={{0}: (6, {}), {1}: (7, {}), {2}: (8, {}), {3}: (9, {})} | custom-call | flops 4294967296 | bytes 16777216 | tf_op jit(solution)/shard_map/pallas_call | solution.py:39
  156.3 4.3 collective-permute-start.14
  162.0 4.6 shard_map.47
  166.6 15.2 %collective-permute-start.20 = (bf16[2,128,1024]{2,1,0:T(8,128)(2,1)S(1)}, bf16[2,128,1024]{2,1,0:T(8,128)(2,1)S(1)}, u32[]{:S(2)}, u32[]{:S(2)}) collective-permute-start(bf16[2,128,1024]{2,1,0:T(8,128)(2,1)S(1)} %get-tuple-element.252), channel_id=1, source_target_pairs={{4,8},{8,12},{20,24},{24,28},{36,40},{40,44},{52,56},{56,60},{68,7... | collective-permute-start | bytes 1572872 | tf_op jit(solution)/shard_map/ppermute | solution.py:376
  181.9 10.1 %collective-permute-start.21 = (bf16[2,128,1024]{2,1,0:T(8,128)(2,1)S(1)}, bf16[2,128,1024]{2,1,0:T(8,128)(2,1)S(1)}, u32[]{:S(2)}, u32[]{:S(2)}) collective-permute-start(bf16[2,128,1024]{2,1,0:T(8,128)(2,1)S(1)} %get-tuple-element.253), channel_id=1, source_target_pairs={{4,0},{8,4},{20,16},{24,20},{36,32},{40,36},{52,48},{56,52},{68,64... | collective-permute-start | bytes 1572872 | tf_op jit(solution)/shard_map/ppermute | solution.py:376
  192.0 4.6 shard_map.48
  196.6 13.0 %collective-permute-start.18 = (bf16[2,128,1024]{2,1,0:T(8,128)(2,1)S(1)}, bf16[2,128,1024]{2,1,0:T(8,128)(2,1)S(1)}, u32[]{:S(2)}, u32[]{:S(2)}) collective-permute-start(bf16[2,128,1024]{2,1,0:T(8,128)(2,1)S(1)} %get-tuple-element.250), channel_id=1, source_target_pairs={{4,8},{8,12},{20,24},{24,28},{36,40},{40,44},{52,56},{56,60},{68,7... | collective-permute-start | bytes 1572872 | tf_op jit(solution)/shard_map/ppermute | solution.py:376
  210.9 4.6 shard_map.49
  215.5 9.6 %collective-permute-start.23 = (bf16[2,128,1024]{2,1,0:T(8,128)(2,1)S(1)}, bf16[2,128,1024]{2,1,0:T(8,128)(2,1)S(1)}, u32[]{:S(2)}, u32[]{:S(2)}) collective-permute-start(bf16[2,128,1024]{2,1,0:T(8,128)(2,1)S(1)} %get-tuple-element.263), channel_id=1, source_target_pairs={{8,12},{24,28},{40,44},{56,60},{72,76},{88,92},{104,108},{120,124}... | collective-permute-start | bytes 1572872 | tf_op jit(solution)/shard_map/ppermute | solution.py:376
  225.1 10.2 %collective-permute-start.24 = (bf16[2,128,1024]{2,1,0:T(8,128)(2,1)S(1)}, bf16[2,128,1024]{2,1,0:T(8,128)(2,1)S(1)}, u32[]{:S(2)}, u32[]{:S(2)}) collective-permute-start(bf16[2,128,1024]{2,1,0:T(8,128)(2,1)S(1)} %get-tuple-element.264), channel_id=1, source_target_pairs={{4,0},{20,16},{36,32},{52,48},{68,64},{84,80},{100,96},{116,112},{... | collective-permute-start | bytes 1572872 | tf_op jit(solution)/shard_map/ppermute | solution.py:376
  235.3 5.4 %shard_map.50 = (bf16[2,1152,1024]{2,1,0:T(8,128)(2,1)S(1)}, bf16[2,1152,1024]{2,1,0:T(8,128)(2,1)S(1)}, bf16[2,1024,1024]{2,1,0:T(8,128)(2,1)S(1)}, bf16[2,1024...) custom-call(s32[3]{0:T(128)S(1)} %pad_add_fusion.place_ref, ...), custom_call_target="tpu_custom_call", output_to_operand_aliasing={{0}: (6, {}), {1}: (7, {}), {2}: (8, {}), {3}: (9, {})} | custom-call | flops 4294967296 | bytes 16777216 | tf_op jit(solution)/shard_map/pallas_call | solution.py:39
  240.7 9.9 %collective-permute-start.22 = (bf16[2,128,1024]{2,1,0:T(8,128)(2,1)S(1)}, bf16[2,128,1024]{2,1,0:T(8,128)(2,1)S(1)}, u32[]{:S(2)}, u32[]{:S(2)}) collective-permute-start(bf16[2,128,1024]{2,1,0:T(8,128)(2,1)S(1)} %get-tuple-element.262), channel_id=1, source_target_pairs={{8,12},{24,28},{40,44},{56,60},{72,76},{88,92},{104,108},{120,124}... | collective-permute-start | bytes 1572872 | tf_op jit(solution)/shard_map/ppermute | solution.py:376
  250.6 5.8 %shard_map.51 = (bf16[2,1152,1024]{2,1,0:T(8,128)(2,1)S(1)}, bf16[2,1152,1024]{2,1,0:T(8,128)(2,1)S(1)}, bf16[2,1024,1024]{2,1,0:T(8,128)(2,1)S(1)}, bf16[2,1024...) custom-call(s32[3]{0:T(128)S(1)} %pad_add_fusion.place_ref, ...), custom_call_target="tpu_custom_call", output_to_operand_aliasing={{0}: (6, {}), {1}: (7, {}), {2}: (8, {}), {3}: (9, {})} | custom-call | flops 4294967296 | bytes 16777216 | tf_op jit(solution)/shard_map/pallas_call | solution.py:39
  268.6 57.1 %collective-permute-start.30 = (bf16[2,32,1024]{2,1,0:T(8,128)(2,1)S(1)}, bf16[2,32,1024]{2,1,0:T(8,128)(2,1)S(1)}, u32[]{:S(2)}, u32[]{:S(2)}) collective-permute-start(bf16[2,32,1024]{2,1,0:T(8,128)(2,1)S(1)} %get-tuple-element.290), channel_id=1, source_target_pairs={{44,60},{60,76},{76,92},{92,108},{45,61},{61,77},{77,93},{93,109},... | collective-permute-start | bytes 393224 | tf_op jit(solution)/shard_map/ppermute | solution.py:413
  326.4 15.9 %collective-permute-start.34 = (bf16[2,32,1024]{2,1,0:T(8,128)(2,1)S(1)}, bf16[2,32,1024]{2,1,0:T(8,128)(2,1)S(1)}, u32[]{:S(2)}, u32[]{:S(2)}) collective-permute-start(bf16[2,32,1024]{2,1,0:T(8,128)(2,1)S(1)} %get-tuple-element.294), channel_id=1, source_target_pairs={{60,76},{76,92},{92,108},{108,124},{61,77},{77,93},{93,109},{109,1... | collective-permute-start | bytes 393224 | tf_op jit(solution)/shard_map/ppermute | solution.py:413
  347.5 4.3 collective-permute-done.31.refs_0_
  353.1 3.7 shard_map.61
  362.0 3.7 shard_map.64
  371.9 3.7 shard_map.67
  378.8 5.4 %collective-permute-done.46.refs_0_ = bf16[2,32,1024]{2,1,0:T(8,128)(2,1)S(1)} collective-permute-done((bf16[2,32,1024]{2,1,0:T(8,128)(2,1)S(1)}, bf16[2,32,1024]{2,1,0:T(8,128)(2,1)S(1)}, u32[]{:S(2)}, u32[]{:S(2)}) %collective-permute-start.46) | collective-permute-done | bytes 131104 | tf_op jit(solution)/shard_map/ppermute | solution.py:416
  384.2 3.7 shard_map.70
  387.9 2.8 collective-permute-done.45.block
  390.7 3.7 shard_map.71
  397.5 7.6 %collective-permute-done.51.block = bf16[2,32,1024]{2,1,0:T(8,128)(2,1)S(1)} collective-permute-done((bf16[2,32,1024]{2,1,0:T(8,128)(2,1)S(1)}, bf16[2,32,1024]{2,1,0:T(8,128)(2,1)S(1)}, u32[]{:S(2)}, u32[]{:S(2)}) %collective-permute-start.51) | collective-permute-done | bytes 131104 | tf_op jit(solution)/shard_map/ppermute | solution.py:456
  405.2 3.7 shard_map.73
  412.0 4.7 collective-permute-done.53.block
  416.7 3.7 shard_map.75
  423.6 3.7 collective-permute-done.55.block
  427.3 4.3 shard_map.77
  432.8 10.7 %collective-permute-start.56 = (bf16[2,32,1024]{2,1,0:T(8,128)(2,1)S(1)}, bf16[2,32,1024]{2,1,0:T(8,128)(2,1)S(1)}, u32[]{:S(2)}, u32[]{:S(2)}) collective-permute-start(bf16[2,32,1024]{2,1,0:T(8,128)(2,1)S(1)} %get-tuple-element.347), channel_id=1, source_target_pairs={{64,48},{80,64},{96,80},{112,96},{65,49},{81,65},{97,81},{113,97},... | collective-permute-start | bytes 393224 | tf_op jit(solution)/shard_map/ppermute | solution.py:467
  444.7 13.9 %collective-permute-start.57 = (bf16[2,32,1024]{2,1,0:T(8,128)(2,1)S(1)}, bf16[2,32,1024]{2,1,0:T(8,128)(2,1)S(1)}, u32[]{:S(2)}, u32[]{:S(2)}) collective-permute-start(bf16[2,32,1024]{2,1,0:T(8,128)(2,1)S(1)} %get-tuple-element.350), channel_id=1, source_target_pairs={{48,32},{64,48},{80,64},{96,80},{49,33},{65,49},{81,65},{97,81},{5... | collective-permute-start | bytes 393224 | tf_op jit(solution)/shard_map/ppermute | solution.py:467
  461.2 12.3 %collective-permute-done.58.block = bf16[2,32,1024]{2,1,0:T(8,128)(2,1)S(1)} collective-permute-done((bf16[2,32,1024]{2,1,0:T(8,128)(2,1)S(1)}, bf16[2,32,1024]{2,1,0:T(8,128)(2,1)S(1)}, u32[]{:S(2)}, u32[]{:S(2)}) %collective-permute-start.58) | collective-permute-done | bytes 131104 | tf_op jit(solution)/shard_map/ppermute | solution.py:467
  475.0 1.9 collective-permute-start.59
  480.9 1.9 collective-permute-done.59.block
  484.4 1.9 collective-permute-start.60
  490.5 4.7 shard_map.86.refs_10_
  495.2 1.6 shard_map.83
  496.8 1.9 collective-permute-start.61
  502.6 4.7 shard_map.87.refs_10_
  507.3 1.6 shard_map.84
  514.2 4.7 shard_map.88.refs_10_
  520.1 4.7 shard_map.89
  524.8 2.0 copy.122
  (148 shorter events, 79.4 us)
Async XLA Ops:
  12.2 36.3 %collective-permute-start = (bf16[2,128,1024]{2,1,0:T(8,128)(2,1)S(1)}, bf16[2,128,1024]{2,1,0:T(8,128)(2,1)S(1)}, u32[]{:S(2)}, u32[]{:S(2)}) collective-permute-start(bf16[2,128,1024]{2,1,0:T(8,128)(2,1)S(1)} %get-tuple-element.192), channel_id=1, source_target_pairs={{0,4},{16,20},{32,36},{48,52},{64,68},{80,84},{96,100},{112,116},{... | collective-permute-start | bytes 1572872 | tf_op jit(solution)/shard_map/ppermute | solution.py:376
  22.8 25.7 %collective-permute-start.1 = (bf16[2,128,1024]{2,1,0:T(8,128)(2,1)S(1)}, bf16[2,128,1024]{2,1,0:T(8,128)(2,1)S(1)}, u32[]{:S(2)}, u32[]{:S(2)}) collective-permute-start(bf16[2,128,1024]{2,1,0:T(8,128)(2,1)S(1)} %get-tuple-element.193), channel_id=1, source_target_pairs={{12,8},{28,24},{44,40},{60,56},{76,72},{92,88},{108,104},{124,120}... | collective-permute-start | bytes 1572872 | tf_op jit(solution)/shard_map/ppermute | solution.py:376
  28.2 36.3 %collective-permute-start.4 = (bf16[2,128,1024]{2,1,0:T(8,128)(2,1)S(1)}, bf16[2,128,1024]{2,1,0:T(8,128)(2,1)S(1)}, u32[]{:S(2)}, u32[]{:S(2)}) collective-permute-start(bf16[2,128,1024]{2,1,0:T(8,128)(2,1)S(1)} %get-tuple-element.204), channel_id=1, source_target_pairs={{0,4},{16,20},{32,36},{48,52},{64,68},{80,84},{96,100},{112,116},{... | collective-permute-start | bytes 1572872 | tf_op jit(solution)/shard_map/ppermute | solution.py:376
  39.6 24.9 %collective-permute-start.5 = (bf16[2,128,1024]{2,1,0:T(8,128)(2,1)S(1)}, bf16[2,128,1024]{2,1,0:T(8,128)(2,1)S(1)}, u32[]{:S(2)}, u32[]{:S(2)}) collective-permute-start(bf16[2,128,1024]{2,1,0:T(8,128)(2,1)S(1)} %get-tuple-element.205), channel_id=1, source_target_pairs={{12,8},{28,24},{44,40},{60,56},{76,72},{92,88},{108,104},{124,120}... | collective-permute-start | bytes 1572872 | tf_op jit(solution)/shard_map/ppermute | solution.py:376
  53.1 36.8 %collective-permute-start.2 = (bf16[2,128,1024]{2,1,0:T(8,128)(2,1)S(1)}, bf16[2,128,1024]{2,1,0:T(8,128)(2,1)S(1)}, u32[]{:S(2)}, u32[]{:S(2)}) collective-permute-start(bf16[2,128,1024]{2,1,0:T(8,128)(2,1)S(1)} %get-tuple-element.202), channel_id=1, source_target_pairs={{0,4},{4,8},{16,20},{20,24},{32,36},{36,40},{48,52},{52,56},{64,68... | collective-permute-start | bytes 1572872 | tf_op jit(solution)/shard_map/ppermute | solution.py:376
  63.7 26.2 %collective-permute-start.3 = (bf16[2,128,1024]{2,1,0:T(8,128)(2,1)S(1)}, bf16[2,128,1024]{2,1,0:T(8,128)(2,1)S(1)}, u32[]{:S(2)}, u32[]{:S(2)}) collective-permute-start(bf16[2,128,1024]{2,1,0:T(8,128)(2,1)S(1)} %get-tuple-element.203), channel_id=1, source_target_pairs={{8,4},{12,8},{24,20},{28,24},{40,36},{44,40},{56,52},{60,56},{72,6... | collective-permute-start | bytes 1572872 | tf_op jit(solution)/shard_map/ppermute | solution.py:376
  69.1 34.2 %collective-permute-start.8 = (bf16[2,128,1024]{2,1,0:T(8,128)(2,1)S(1)}, bf16[2,128,1024]{2,1,0:T(8,128)(2,1)S(1)}, u32[]{:S(2)}, u32[]{:S(2)}) collective-permute-start(bf16[2,128,1024]{2,1,0:T(8,128)(2,1)S(1)} %get-tuple-element.216), channel_id=1, source_target_pairs={{0,4},{4,8},{16,20},{20,24},{32,36},{36,40},{48,52},{52,56},{64,68... | collective-permute-start | bytes 1572872 | tf_op jit(solution)/shard_map/ppermute | solution.py:376
  81.0 22.2 %collective-permute-start.9 = (bf16[2,128,1024]{2,1,0:T(8,128)(2,1)S(1)}, bf16[2,128,1024]{2,1,0:T(8,128)(2,1)S(1)}, u32[]{:S(2)}, u32[]{:S(2)}) collective-permute-start(bf16[2,128,1024]{2,1,0:T(8,128)(2,1)S(1)} %get-tuple-element.217), channel_id=1, source_target_pairs={{8,4},{12,8},{24,20},{28,24},{40,36},{44,40},{56,52},{60,56},{72,6... | collective-permute-start | bytes 1572872 | tf_op jit(solution)/shard_map/ppermute | solution.py:376
  94.6 23.3 %collective-permute-start.6 = (bf16[2,128,1024]{2,1,0:T(8,128)(2,1)S(1)}, bf16[2,128,1024]{2,1,0:T(8,128)(2,1)S(1)}, u32[]{:S(2)}, u32[]{:S(2)}) collective-permute-start(bf16[2,128,1024]{2,1,0:T(8,128)(2,1)S(1)} %get-tuple-element.214), channel_id=1, source_target_pairs={{0,4},{4,8},{8,12},{16,20},{20,24},{24,28},{32,36},{36,40},{40,44}... | collective-permute-start | bytes 1572872 | tf_op jit(solution)/shard_map/ppermute | solution.py:376
  101.9 15.9 %collective-permute-start.7 = (bf16[2,128,1024]{2,1,0:T(8,128)(2,1)S(1)}, bf16[2,128,1024]{2,1,0:T(8,128)(2,1)S(1)}, u32[]{:S(2)}, u32[]{:S(2)}) collective-permute-start(bf16[2,128,1024]{2,1,0:T(8,128)(2,1)S(1)} %get-tuple-element.215), channel_id=1, source_target_pairs={{4,0},{8,4},{12,8},{20,16},{24,20},{28,24},{36,32},{40,36},{44,40}... | collective-permute-start | bytes 1572872 | tf_op jit(solution)/shard_map/ppermute | solution.py:376
  107.9 25.0 %collective-permute-start.12 = (bf16[2,128,1024]{2,1,0:T(8,128)(2,1)S(1)}, bf16[2,128,1024]{2,1,0:T(8,128)(2,1)S(1)}, u32[]{:S(2)}, u32[]{:S(2)}) collective-permute-start(bf16[2,128,1024]{2,1,0:T(8,128)(2,1)S(1)} %get-tuple-element.228), channel_id=1, source_target_pairs={{0,4},{4,8},{8,12},{16,20},{20,24},{24,28},{32,36},{36,40},{40,44}... | collective-permute-start | bytes 1572872 | tf_op jit(solution)/shard_map/ppermute | solution.py:376
  116.6 16.3 %collective-permute-start.13 = (bf16[2,128,1024]{2,1,0:T(8,128)(2,1)S(1)}, bf16[2,128,1024]{2,1,0:T(8,128)(2,1)S(1)}, u32[]{:S(2)}, u32[]{:S(2)}) collective-permute-start(bf16[2,128,1024]{2,1,0:T(8,128)(2,1)S(1)} %get-tuple-element.229), channel_id=1, source_target_pairs={{4,0},{8,4},{12,8},{20,16},{24,20},{28,24},{36,32},{40,36},{44,40}... | collective-permute-start | bytes 1572872 | tf_op jit(solution)/shard_map/ppermute | solution.py:376
  127.0 20.4 %collective-permute-start.10 = (bf16[2,128,1024]{2,1,0:T(8,128)(2,1)S(1)}, bf16[2,128,1024]{2,1,0:T(8,128)(2,1)S(1)}, u32[]{:S(2)}, u32[]{:S(2)}) collective-permute-start(bf16[2,128,1024]{2,1,0:T(8,128)(2,1)S(1)} %get-tuple-element.226), channel_id=1, source_target_pairs={{0,4},{4,8},{8,12},{16,20},{20,24},{24,28},{32,36},{36,40},{40,44}... | collective-permute-start | bytes 1572872 | tf_op jit(solution)/shard_map/ppermute | solution.py:376
  131.6 15.9 %collective-permute-start.11 = (bf16[2,128,1024]{2,1,0:T(8,128)(2,1)S(1)}, bf16[2,128,1024]{2,1,0:T(8,128)(2,1)S(1)}, u32[]{:S(2)}, u32[]{:S(2)}) collective-permute-start(bf16[2,128,1024]{2,1,0:T(8,128)(2,1)S(1)} %get-tuple-element.227), channel_id=1, source_target_pairs={{4,0},{8,4},{12,8},{20,16},{24,20},{28,24},{36,32},{40,36},{44,40}... | collective-permute-start | bytes 1572872 | tf_op jit(solution)/shard_map/ppermute | solution.py:376
  141.5 20.4 %collective-permute-start.16 = (bf16[2,128,1024]{2,1,0:T(8,128)(2,1)S(1)}, bf16[2,128,1024]{2,1,0:T(8,128)(2,1)S(1)}, u32[]{:S(2)}, u32[]{:S(2)}) collective-permute-start(bf16[2,128,1024]{2,1,0:T(8,128)(2,1)S(1)} %get-tuple-element.240), channel_id=1, source_target_pairs={{0,4},{4,8},{8,12},{16,20},{20,24},{24,28},{32,36},{36,40},{40,44}... | collective-permute-start | bytes 1572872 | tf_op jit(solution)/shard_map/ppermute | solution.py:376
  146.1 15.9 %collective-permute-start.17 = (bf16[2,128,1024]{2,1,0:T(8,128)(2,1)S(1)}, bf16[2,128,1024]{2,1,0:T(8,128)(2,1)S(1)}, u32[]{:S(2)}, u32[]{:S(2)}) collective-permute-start(bf16[2,128,1024]{2,1,0:T(8,128)(2,1)S(1)} %get-tuple-element.241), channel_id=1, source_target_pairs={{4,0},{8,4},{12,8},{20,16},{24,20},{28,24},{36,32},{40,36},{44,40}... | collective-permute-start | bytes 1572872 | tf_op jit(solution)/shard_map/ppermute | solution.py:376
  156.3 35.7 %collective-permute-start.14 = (bf16[2,128,1024]{2,1,0:T(8,128)(2,1)S(1)}, bf16[2,128,1024]{2,1,0:T(8,128)(2,1)S(1)}, u32[]{:S(2)}, u32[]{:S(2)}) collective-permute-start(bf16[2,128,1024]{2,1,0:T(8,128)(2,1)S(1)} %get-tuple-element.238), channel_id=1, source_target_pairs={{0,4},{4,8},{8,12},{16,20},{20,24},{24,28},{32,36},{36,40},{40,44}... | collective-permute-start | bytes 1572872 | tf_op jit(solution)/shard_map/ppermute | solution.py:376
  160.7 31.3 %collective-permute-start.15 = (bf16[2,128,1024]{2,1,0:T(8,128)(2,1)S(1)}, bf16[2,128,1024]{2,1,0:T(8,128)(2,1)S(1)}, u32[]{:S(2)}, u32[]{:S(2)}) collective-permute-start(bf16[2,128,1024]{2,1,0:T(8,128)(2,1)S(1)} %get-tuple-element.239), channel_id=1, source_target_pairs={{4,0},{8,4},{20,16},{24,20},{36,32},{40,36},{52,48},{56,52},{68,64... | collective-permute-start | bytes 1572872 | tf_op jit(solution)/shard_map/ppermute | solution.py:376
  166.6 44.3 %collective-permute-start.20 = (bf16[2,128,1024]{2,1,0:T(8,128)(2,1)S(1)}, bf16[2,128,1024]{2,1,0:T(8,128)(2,1)S(1)}, u32[]{:S(2)}, u32[]{:S(2)}) collective-permute-start(bf16[2,128,1024]{2,1,0:T(8,128)(2,1)S(1)} %get-tuple-element.252), channel_id=1, source_target_pairs={{4,8},{8,12},{20,24},{24,28},{36,40},{40,44},{52,56},{56,60},{68,7... | collective-permute-start | bytes 1572872 | tf_op jit(solution)/shard_map/ppermute | solution.py:376
  181.9 29.1 %collective-permute-start.21 = (bf16[2,128,1024]{2,1,0:T(8,128)(2,1)S(1)}, bf16[2,128,1024]{2,1,0:T(8,128)(2,1)S(1)}, u32[]{:S(2)}, u32[]{:S(2)}) collective-permute-start(bf16[2,128,1024]{2,1,0:T(8,128)(2,1)S(1)} %get-tuple-element.253), channel_id=1, source_target_pairs={{4,0},{8,4},{20,16},{24,20},{36,32},{40,36},{52,48},{56,52},{68,64... | collective-permute-start | bytes 1572872 | tf_op jit(solution)/shard_map/ppermute | solution.py:376
  196.6 38.7 %collective-permute-start.18 = (bf16[2,128,1024]{2,1,0:T(8,128)(2,1)S(1)}, bf16[2,128,1024]{2,1,0:T(8,128)(2,1)S(1)}, u32[]{:S(2)}, u32[]{:S(2)}) collective-permute-start(bf16[2,128,1024]{2,1,0:T(8,128)(2,1)S(1)} %get-tuple-element.250), channel_id=1, source_target_pairs={{4,8},{8,12},{20,24},{24,28},{36,40},{40,44},{52,56},{56,60},{68,7... | collective-permute-start | bytes 1572872 | tf_op jit(solution)/shard_map/ppermute | solution.py:376
  209.6 25.7 %collective-permute-start.19 = (bf16[2,128,1024]{2,1,0:T(8,128)(2,1)S(1)}, bf16[2,128,1024]{2,1,0:T(8,128)(2,1)S(1)}, u32[]{:S(2)}, u32[]{:S(2)}) collective-permute-start(bf16[2,128,1024]{2,1,0:T(8,128)(2,1)S(1)} %get-tuple-element.251), channel_id=1, source_target_pairs={{4,0},{20,16},{36,32},{52,48},{68,64},{84,80},{100,96},{116,112},{... | collective-permute-start | bytes 1572872 | tf_op jit(solution)/shard_map/ppermute | solution.py:376
  215.5 35.0 %collective-permute-start.23 = (bf16[2,128,1024]{2,1,0:T(8,128)(2,1)S(1)}, bf16[2,128,1024]{2,1,0:T(8,128)(2,1)S(1)}, u32[]{:S(2)}, u32[]{:S(2)}) collective-permute-start(bf16[2,128,1024]{2,1,0:T(8,128)(2,1)S(1)} %get-tuple-element.263), channel_id=1, source_target_pairs={{8,12},{24,28},{40,44},{56,60},{72,76},{88,92},{104,108},{120,124}... | collective-permute-start | bytes 1572872 | tf_op jit(solution)/shard_map/ppermute | solution.py:376
  225.1 25.5 %collective-permute-start.24 = (bf16[2,128,1024]{2,1,0:T(8,128)(2,1)S(1)}, bf16[2,128,1024]{2,1,0:T(8,128)(2,1)S(1)}, u32[]{:S(2)}, u32[]{:S(2)}) collective-permute-start(bf16[2,128,1024]{2,1,0:T(8,128)(2,1)S(1)} %get-tuple-element.264), channel_id=1, source_target_pairs={{4,0},{20,16},{36,32},{52,48},{68,64},{84,80},{100,96},{116,112},{... | collective-permute-start | bytes 1572872 | tf_op jit(solution)/shard_map/ppermute | solution.py:376
  240.7 15.6 %collective-permute-start.22 = (bf16[2,128,1024]{2,1,0:T(8,128)(2,1)S(1)}, bf16[2,128,1024]{2,1,0:T(8,128)(2,1)S(1)}, u32[]{:S(2)}, u32[]{:S(2)}) collective-permute-start(bf16[2,128,1024]{2,1,0:T(8,128)(2,1)S(1)} %get-tuple-element.262), channel_id=1, source_target_pairs={{8,12},{24,28},{40,44},{56,60},{72,76},{88,92},{104,108},{120,124}... | collective-permute-start | bytes 1572872 | tf_op jit(solution)/shard_map/ppermute | solution.py:376
  268.6 57.1 %collective-permute-start.30 = (bf16[2,32,1024]{2,1,0:T(8,128)(2,1)S(1)}, bf16[2,32,1024]{2,1,0:T(8,128)(2,1)S(1)}, u32[]{:S(2)}, u32[]{:S(2)}) collective-permute-start(bf16[2,32,1024]{2,1,0:T(8,128)(2,1)S(1)} %get-tuple-element.290), channel_id=1, source_target_pairs={{44,60},{60,76},{76,92},{92,108},{45,61},{61,77},{77,93},{93,109},... | collective-permute-start | bytes 393224 | tf_op jit(solution)/shard_map/ppermute | solution.py:413
  326.4 18.6 %collective-permute-start.34 = (bf16[2,32,1024]{2,1,0:T(8,128)(2,1)S(1)}, bf16[2,32,1024]{2,1,0:T(8,128)(2,1)S(1)}, u32[]{:S(2)}, u32[]{:S(2)}) collective-permute-start(bf16[2,32,1024]{2,1,0:T(8,128)(2,1)S(1)} %get-tuple-element.294), channel_id=1, source_target_pairs={{60,76},{76,92},{92,108},{108,124},{61,77},{77,93},{93,109},{109,1... | collective-permute-start | bytes 393224 | tf_op jit(solution)/shard_map/ppermute | solution.py:413
  342.2 9.5 %collective-permute-start.31 = (bf16[2,32,1024]{2,1,0:T(8,128)(2,1)S(1)}, bf16[2,32,1024]{2,1,0:T(8,128)(2,1)S(1)}, u32[]{:S(2)}, u32[]{:S(2)}) collective-permute-start(bf16[2,32,1024]{2,1,0:T(8,128)(2,1)S(1)} %get-tuple-element.293), channel_id=1, source_target_pairs={{12,16},{28,32},{44,48},{60,64},{76,80},{92,96},{108,112},{13,17},... | collective-permute-start | bytes 393224 | tf_op jit(solution)/shard_map/ppermute | solution.py:416
  343.5 8.9 %collective-permute-start.32 = (bf16[2,32,1024]{2,1,0:T(8,128)(2,1)S(1)}, bf16[2,32,1024]{2,1,0:T(8,128)(2,1)S(1)}, u32[]{:S(2)}, u32[]{:S(2)}) collective-permute-start(bf16[2,32,1024]{2,1,0:T(8,128)(2,1)S(1)} %get-tuple-element.293), channel_id=1, source_target_pairs={{12,20},{28,36},{44,52},{60,68},{76,84},{92,100},{108,116},{13,21}... | collective-permute-start | bytes 393224 | tf_op jit(solution)/shard_map/ppermute | solution.py:416
  344.2 8.9 %collective-permute-start.33 = (bf16[2,32,1024]{2,1,0:T(8,128)(2,1)S(1)}, bf16[2,32,1024]{2,1,0:T(8,128)(2,1)S(1)}, u32[]{:S(2)}, u32[]{:S(2)}) collective-permute-start(bf16[2,32,1024]{2,1,0:T(8,128)(2,1)S(1)} %get-tuple-element.293), channel_id=1, source_target_pairs={{12,24},{28,40},{44,56},{60,72},{76,88},{92,104},{108,120},{13,25}... | collective-permute-start | bytes 393224 | tf_op jit(solution)/shard_map/ppermute | solution.py:416
  345.5 14.5 %collective-permute-start.36 = (bf16[2,32,1024]{2,1,0:T(8,128)(2,1)S(1)}, bf16[2,32,1024]{2,1,0:T(8,128)(2,1)S(1)}, u32[]{:S(2)}, u32[]{:S(2)}) collective-permute-start(bf16[2,32,1024]{2,1,0:T(8,128)(2,1)S(1)} %get-tuple-element.302), channel_id=1, source_target_pairs={{12,16},{28,32},{44,48},{60,64},{76,80},{92,96},{108,112},{13,17},... | collective-permute-start | bytes 393224 | tf_op jit(solution)/shard_map/ppermute | solution.py:416
  346.8 13.9 %collective-permute-start.37 = (bf16[2,32,1024]{2,1,0:T(8,128)(2,1)S(1)}, bf16[2,32,1024]{2,1,0:T(8,128)(2,1)S(1)}, u32[]{:S(2)}, u32[]{:S(2)}) collective-permute-start(bf16[2,32,1024]{2,1,0:T(8,128)(2,1)S(1)} %get-tuple-element.302), channel_id=1, source_target_pairs={{12,20},{28,36},{44,52},{60,68},{76,84},{92,100},{108,116},{13,21}... | collective-permute-start | bytes 393224 | tf_op jit(solution)/shard_map/ppermute | solution.py:416
  351.8 9.6 %collective-permute-start.38 = (bf16[2,32,1024]{2,1,0:T(8,128)(2,1)S(1)}, bf16[2,32,1024]{2,1,0:T(8,128)(2,1)S(1)}, u32[]{:S(2)}, u32[]{:S(2)}) collective-permute-start(bf16[2,32,1024]{2,1,0:T(8,128)(2,1)S(1)} %get-tuple-element.302), channel_id=1, source_target_pairs={{12,24},{28,40},{44,56},{60,72},{76,88},{92,104},{108,120},{13,25}... | collective-permute-start | bytes 393224 | tf_op jit(solution)/shard_map/ppermute | solution.py:416
  357.4 8.4 %collective-permute-start.35 = (bf16[2,32,1024]{2,1,0:T(8,128)(2,1)S(1)}, bf16[2,32,1024]{2,1,0:T(8,128)(2,1)S(1)}, u32[]{:S(2)}, u32[]{:S(2)}) collective-permute-start(bf16[2,32,1024]{2,1,0:T(8,128)(2,1)S(1)} %get-tuple-element.301), channel_id=1, source_target_pairs={{12,8},{28,24},{44,40},{60,56},{76,72},{92,88},{108,104},{124,120}... | collective-permute-start | bytes 393224 | tf_op jit(solution)/shard_map/ppermute | solution.py:456
  358.7 11.2 %collective-permute-start.41 = (bf16[2,32,1024]{2,1,0:T(8,128)(2,1)S(1)}, bf16[2,32,1024]{2,1,0:T(8,128)(2,1)S(1)}, u32[]{:S(2)}, u32[]{:S(2)}) collective-permute-start(bf16[2,32,1024]{2,1,0:T(8,128)(2,1)S(1)} %get-tuple-element.311), channel_id=1, source_target_pairs={{12,16},{28,32},{44,48},{60,64},{76,80},{92,96},{108,112},{13,17},... | collective-permute-start | bytes 393224 | tf_op jit(solution)/shard_map/ppermute | solution.py:416
  360.0 10.6 %collective-permute-start.42 = (bf16[2,32,1024]{2,1,0:T(8,128)(2,1)S(1)}, bf16[2,32,1024]{2,1,0:T(8,128)(2,1)S(1)}, u32[]{:S(2)}, u32[]{:S(2)}) collective-permute-start(bf16[2,32,1024]{2,1,0:T(8,128)(2,1)S(1)} %get-tuple-element.311), channel_id=1, source_target_pairs={{12,20},{28,36},{44,52},{60,68},{76,84},{92,100},{108,116},{13,21}... | collective-permute-start | bytes 393224 | tf_op jit(solution)/shard_map/ppermute | solution.py:416
  360.7 10.6 %collective-permute-start.43 = (bf16[2,32,1024]{2,1,0:T(8,128)(2,1)S(1)}, bf16[2,32,1024]{2,1,0:T(8,128)(2,1)S(1)}, u32[]{:S(2)}, u32[]{:S(2)}) collective-permute-start(bf16[2,32,1024]{2,1,0:T(8,128)(2,1)S(1)} %get-tuple-element.311), channel_id=1, source_target_pairs={{12,24},{28,40},{44,56},{60,72},{76,88},{92,104},{108,120},{13,25}... | collective-permute-start | bytes 393224 | tf_op jit(solution)/shard_map/ppermute | solution.py:416
  366.3 9.3 %collective-permute-start.40 = (bf16[2,32,1024]{2,1,0:T(8,128)(2,1)S(1)}, bf16[2,32,1024]{2,1,0:T(8,128)(2,1)S(1)}, u32[]{:S(2)}, u32[]{:S(2)}) collective-permute-start(bf16[2,32,1024]{2,1,0:T(8,128)(2,1)S(1)} %get-tuple-element.310), channel_id=1, source_target_pairs={{8,4},{12,8},{24,20},{28,24},{40,36},{44,40},{56,52},{60,56},{72,6... | collective-permute-start | bytes 393224 | tf_op jit(solution)/shard_map/ppermute | solution.py:456
  367.8 16.4 %collective-permute-start.46 = (bf16[2,32,1024]{2,1,0:T(8,128)(2,1)S(1)}, bf16[2,32,1024]{2,1,0:T(8,128)(2,1)S(1)}, u32[]{:S(2)}, u32[]{:S(2)}) collective-permute-start(bf16[2,32,1024]{2,1,0:T(8,128)(2,1)S(1)} %get-tuple-element.320), channel_id=1, source_target_pairs={{12,16},{28,32},{44,48},{60,64},{76,80},{92,96},{108,112},{13,17},... | collective-permute-start | bytes 393224 | tf_op jit(solution)/shard_map/ppermute | solution.py:416
  369.9 14.3 %collective-permute-start.47 = (bf16[2,32,1024]{2,1,0:T(8,128)(2,1)S(1)}, bf16[2,32,1024]{2,1,0:T(8,128)(2,1)S(1)}, u32[]{:S(2)}, u32[]{:S(2)}) collective-permute-start(bf16[2,32,1024]{2,1,0:T(8,128)(2,1)S(1)} %get-tuple-element.320), channel_id=1, source_target_pairs={{12,20},{28,36},{44,52},{60,68},{76,84},{92,100},{108,116},{13,21}... | collective-permute-start | bytes 393224 | tf_op jit(solution)/shard_map/ppermute | solution.py:416
  370.6 13.6 %collective-permute-start.48 = (bf16[2,32,1024]{2,1,0:T(8,128)(2,1)S(1)}, bf16[2,32,1024]{2,1,0:T(8,128)(2,1)S(1)}, u32[]{:S(2)}, u32[]{:S(2)}) collective-permute-start(bf16[2,32,1024]{2,1,0:T(8,128)(2,1)S(1)} %get-tuple-element.320), channel_id=1, source_target_pairs={{12,24},{28,40},{44,56},{60,72},{76,88},{92,104},{108,120},{13,25}... | collective-permute-start | bytes 393224 | tf_op jit(solution)/shard_map/ppermute | solution.py:416
  376.2 14.5 %collective-permute-start.45 = (bf16[2,32,1024]{2,1,0:T(8,128)(2,1)S(1)}, bf16[2,32,1024]{2,1,0:T(8,128)(2,1)S(1)}, u32[]{:S(2)}, u32[]{:S(2)}) collective-permute-start(bf16[2,32,1024]{2,1,0:T(8,128)(2,1)S(1)} %get-tuple-element.319), channel_id=1, source_target_pairs={{4,0},{8,4},{12,8},{20,16},{24,20},{28,24},{36,32},{40,36},{44,40}... | collective-permute-start | bytes 393224 | tf_op jit(solution)/shard_map/ppermute | solution.py:456
  394.4 10.8 %collective-permute-start.51 = (bf16[2,32,1024]{2,1,0:T(8,128)(2,1)S(1)}, bf16[2,32,1024]{2,1,0:T(8,128)(2,1)S(1)}, u32[]{:S(2)}, u32[]{:S(2)}) collective-permute-start(bf16[2,32,1024]{2,1,0:T(8,128)(2,1)S(1)} %get-tuple-element.330), channel_id=1, source_target_pairs={{4,0},{8,4},{12,8},{20,16},{24,20},{28,24},{36,32},{40,36},{44,40}... | collective-permute-start | bytes 393224 | tf_op jit(solution)/shard_map/ppermute | solution.py:456
  396.9 13.3 %collective-permute-start.50 = (bf16[2,32,1024]{2,1,0:T(8,128)(2,1)S(1)}, bf16[2,32,1024]{2,1,0:T(8,128)(2,1)S(1)}, u32[]{:S(2)}, u32[]{:S(2)}) collective-permute-start(bf16[2,32,1024]{2,1,0:T(8,128)(2,1)S(1)} %get-tuple-element.329), channel_id=1, source_target_pairs={{112,96},{113,97},{114,98},{115,99}} | collective-permute-start | bytes 393224 | tf_op jit(solution)/shard_map/ppermute | solution.py:467
  408.8 7.9 %collective-permute-start.53 = (bf16[2,32,1024]{2,1,0:T(8,128)(2,1)S(1)}, bf16[2,32,1024]{2,1,0:T(8,128)(2,1)S(1)}, u32[]{:S(2)}, u32[]{:S(2)}) collective-permute-start(bf16[2,32,1024]{2,1,0:T(8,128)(2,1)S(1)} %get-tuple-element.336), channel_id=1, source_target_pairs={{4,0},{8,4},{20,16},{24,20},{36,32},{40,36},{52,48},{56,52},{68,64... | collective-permute-start | bytes 393224 | tf_op jit(solution)/shard_map/ppermute | solution.py:456
  411.4 10.4 %collective-permute-start.52 = (bf16[2,32,1024]{2,1,0:T(8,128)(2,1)S(1)}, bf16[2,32,1024]{2,1,0:T(8,128)(2,1)S(1)}, u32[]{:S(2)}, u32[]{:S(2)}) collective-permute-start(bf16[2,32,1024]{2,1,0:T(8,128)(2,1)S(1)} %get-tuple-element.335), channel_id=1, source_target_pairs={{96,80},{112,96},{97,81},{113,97},{98,82},{114,98},{99,83},{115,99}} | collective-permute-start | bytes 393224 | tf_op jit(solution)/shard_map/ppermute | solution.py:467
  422.9 8.7 %collective-permute-start.54 = (bf16[2,32,1024]{2,1,0:T(8,128)(2,1)S(1)}, bf16[2,32,1024]{2,1,0:T(8,128)(2,1)S(1)}, u32[]{:S(2)}, u32[]{:S(2)}) collective-permute-start(bf16[2,32,1024]{2,1,0:T(8,128)(2,1)S(1)} %get-tuple-element.341), channel_id=1, source_target_pairs={{80,64},{96,80},{112,96},{81,65},{97,81},{113,97},{82,66},{98,82},... | collective-permute-start | bytes 393224 | tf_op jit(solution)/shard_map/ppermute | solution.py:467
  432.8 10.7 %collective-permute-start.56 = (bf16[2,32,1024]{2,1,0:T(8,128)(2,1)S(1)}, bf16[2,32,1024]{2,1,0:T(8,128)(2,1)S(1)}, u32[]{:S(2)}, u32[]{:S(2)}) collective-permute-start(bf16[2,32,1024]{2,1,0:T(8,128)(2,1)S(1)} %get-tuple-element.347), channel_id=1, source_target_pairs={{64,48},{80,64},{96,80},{112,96},{65,49},{81,65},{97,81},{113,97},... | collective-permute-start | bytes 393224 | tf_op jit(solution)/shard_map/ppermute | solution.py:467
  444.7 13.9 %collective-permute-start.57 = (bf16[2,32,1024]{2,1,0:T(8,128)(2,1)S(1)}, bf16[2,32,1024]{2,1,0:T(8,128)(2,1)S(1)}, u32[]{:S(2)}, u32[]{:S(2)}) collective-permute-start(bf16[2,32,1024]{2,1,0:T(8,128)(2,1)S(1)} %get-tuple-element.350), channel_id=1, source_target_pairs={{48,32},{64,48},{80,64},{96,80},{49,33},{65,49},{81,65},{97,81},{5... | collective-permute-start | bytes 393224 | tf_op jit(solution)/shard_map/ppermute | solution.py:467
  459.9 13.6 %collective-permute-start.58 = (bf16[2,32,1024]{2,1,0:T(8,128)(2,1)S(1)}, bf16[2,32,1024]{2,1,0:T(8,128)(2,1)S(1)}, u32[]{:S(2)}, u32[]{:S(2)}) collective-permute-start(bf16[2,32,1024]{2,1,0:T(8,128)(2,1)S(1)} %get-tuple-element.353), channel_id=1, source_target_pairs={{32,16},{48,32},{64,48},{80,64},{33,17},{49,33},{65,49},{81,65},{3... | collective-permute-start | bytes 393224 | tf_op jit(solution)/shard_map/ppermute | solution.py:467
  477.0 10.6 %collective-permute-start.72 = (bf16[2,32,1024]{2,1,0:T(8,128)(2,1)S(1)}, bf16[2,32,1024]{2,1,0:T(8,128)(2,1)S(1)}, u32[]{:S(2)}, u32[]{:S(2)}) collective-permute-start(bf16[2,32,1024]{2,1,0:T(8,128)(2,1)S(1)} %get-tuple-element.374), channel_id=1, source_target_pairs={{16,4},{32,20},{48,36},{64,52},{80,68},{96,84},{112,100},{17,5},{3... | collective-permute-start | bytes 393224 | tf_op jit(solution)/shard_map/ppermute | solution.py:470
  478.3 10.9 %collective-permute-start.73 = (bf16[2,32,1024]{2,1,0:T(8,128)(2,1)S(1)}, bf16[2,32,1024]{2,1,0:T(8,128)(2,1)S(1)}, u32[]{:S(2)}, u32[]{:S(2)}) collective-permute-start(bf16[2,32,1024]{2,1,0:T(8,128)(2,1)S(1)} %get-tuple-element.374), channel_id=1, source_target_pairs={{16,8},{32,24},{48,40},{64,56},{80,72},{96,88},{112,104},{17,9},{3... | collective-permute-start | bytes 393224 | tf_op jit(solution)/shard_map/ppermute | solution.py:470
  479.6 10.9 %collective-permute-start.74 = (bf16[2,32,1024]{2,1,0:T(8,128)(2,1)S(1)}, bf16[2,32,1024]{2,1,0:T(8,128)(2,1)S(1)}, u32[]{:S(2)}, u32[]{:S(2)}) collective-permute-start(bf16[2,32,1024]{2,1,0:T(8,128)(2,1)S(1)} %get-tuple-element.374), channel_id=1, source_target_pairs={{16,12},{32,28},{48,44},{64,60},{80,76},{96,92},{112,108},{17,13},... | collective-permute-start | bytes 393224 | tf_op jit(solution)/shard_map/ppermute | solution.py:470
  484.4 10.8 %collective-permute-start.60 = (bf16[2,32,1024]{2,1,0:T(8,128)(2,1)S(1)}, bf16[2,32,1024]{2,1,0:T(8,128)(2,1)S(1)}, u32[]{:S(2)}, u32[]{:S(2)}) collective-permute-start(bf16[2,32,1024]{2,1,0:T(8,128)(2,1)S(1)} %get-tuple-element.359), channel_id=1, source_target_pairs={{16,0},{32,16},{48,32},{17,1},{33,17},{49,33},{18,2},{34,18},{50,3... | collective-permute-start | bytes 393224 | tf_op jit(solution)/shard_map/ppermute | solution.py:467
  486.3 13.7 %collective-permute-start.69 = (bf16[2,32,1024]{2,1,0:T(8,128)(2,1)S(1)}, bf16[2,32,1024]{2,1,0:T(8,128)(2,1)S(1)}, u32[]{:S(2)}, u32[]{:S(2)}) collective-permute-start(bf16[2,32,1024]{2,1,0:T(8,128)(2,1)S(1)} %get-tuple-element.373), channel_id=1, source_target_pairs={{16,4},{32,20},{48,36},{64,52},{80,68},{96,84},{112,100},{17,5},{3... | collective-permute-start | bytes 393224 | tf_op jit(solution)/shard_map/ppermute | solution.py:470
  487.6 13.7 %collective-permute-start.70 = (bf16[2,32,1024]{2,1,0:T(8,128)(2,1)S(1)}, bf16[2,32,1024]{2,1,0:T(8,128)(2,1)S(1)}, u32[]{:S(2)}, u32[]{:S(2)}) collective-permute-start(bf16[2,32,1024]{2,1,0:T(8,128)(2,1)S(1)} %get-tuple-element.373), channel_id=1, source_target_pairs={{16,8},{32,24},{48,40},{64,56},{80,72},{96,88},{112,104},{17,9},{3... | collective-permute-start | bytes 393224 | tf_op jit(solution)/shard_map/ppermute | solution.py:470
  489.2 13.4 %collective-permute-start.71 = (bf16[2,32,1024]{2,1,0:T(8,128)(2,1)S(1)}, bf16[2,32,1024]{2,1,0:T(8,128)(2,1)S(1)}, u32[]{:S(2)}, u32[]{:S(2)}) collective-permute-start(bf16[2,32,1024]{2,1,0:T(8,128)(2,1)S(1)} %get-tuple-element.373), channel_id=1, source_target_pairs={{16,12},{32,28},{48,44},{64,60},{80,76},{96,92},{112,108},{17,13},... | collective-permute-start | bytes 393224 | tf_op jit(solution)/shard_map/ppermute | solution.py:470
  496.8 10.5 %collective-permute-start.61 = (bf16[2,32,1024]{2,1,0:T(8,128)(2,1)S(1)}, bf16[2,32,1024]{2,1,0:T(8,128)(2,1)S(1)}, u32[]{:S(2)}, u32[]{:S(2)}) collective-permute-start(bf16[2,32,1024]{2,1,0:T(8,128)(2,1)S(1)} %get-tuple-element.362), channel_id=1, source_target_pairs={{16,0},{32,16},{17,1},{33,17},{18,2},{34,18},{19,3},{35,19}} | collective-permute-start | bytes 393224 | tf_op jit(solution)/shard_map/ppermute | solution.py:467
  498.7 12.8 %collective-permute-start.66 = (bf16[2,32,1024]{2,1,0:T(8,128)(2,1)S(1)}, bf16[2,32,1024]{2,1,0:T(8,128)(2,1)S(1)}, u32[]{:S(2)}, u32[]{:S(2)}) collective-permute-start(bf16[2,32,1024]{2,1,0:T(8,128)(2,1)S(1)} %get-tuple-element.372), channel_id=1, source_target_pairs={{16,4},{32,20},{48,36},{64,52},{80,68},{96,84},{112,100},{17,5},{3... | collective-permute-start | bytes 393224 | tf_op jit(solution)/shard_map/ppermute | solution.py:470
  500.0 12.8 %collective-permute-start.67 = (bf16[2,32,1024]{2,1,0:T(8,128)(2,1)S(1)}, bf16[2,32,1024]{2,1,0:T(8,128)(2,1)S(1)}, u32[]{:S(2)}, u32[]{:S(2)}) collective-permute-start(bf16[2,32,1024]{2,1,0:T(8,128)(2,1)S(1)} %get-tuple-element.372), channel_id=1, source_target_pairs={{16,8},{32,24},{48,40},{64,56},{80,72},{96,88},{112,104},{17,9},{3... | collective-permute-start | bytes 393224 | tf_op jit(solution)/shard_map/ppermute | solution.py:470
  501.3 12.8 %collective-permute-start.68 = (bf16[2,32,1024]{2,1,0:T(8,128)(2,1)S(1)}, bf16[2,32,1024]{2,1,0:T(8,128)(2,1)S(1)}, u32[]{:S(2)}, u32[]{:S(2)}) collective-permute-start(bf16[2,32,1024]{2,1,0:T(8,128)(2,1)S(1)} %get-tuple-element.372), channel_id=1, source_target_pairs={{16,12},{32,28},{48,44},{64,60},{80,76},{96,92},{112,108},{17,13},... | collective-permute-start | bytes 393224 | tf_op jit(solution)/shard_map/ppermute | solution.py:470
  508.9 9.9 %collective-permute-start.65 = (bf16[2,32,1024]{2,1,0:T(8,128)(2,1)S(1)}, bf16[2,32,1024]{2,1,0:T(8,128)(2,1)S(1)}, u32[]{:S(2)}, u32[]{:S(2)}) collective-permute-start(bf16[2,32,1024]{2,1,0:T(8,128)(2,1)S(1)} %get-tuple-element.366), channel_id=1, source_target_pairs={{16,0},{17,1},{18,2},{19,3}} | collective-permute-start | bytes 393224 | tf_op jit(solution)/shard_map/ppermute | solution.py:467
  510.2 9.9 %collective-permute-start.62 = (bf16[2,32,1024]{2,1,0:T(8,128)(2,1)S(1)}, bf16[2,32,1024]{2,1,0:T(8,128)(2,1)S(1)}, u32[]{:S(2)}, u32[]{:S(2)}) collective-permute-start(bf16[2,32,1024]{2,1,0:T(8,128)(2,1)S(1)} %get-tuple-element.365), channel_id=1, source_target_pairs={{16,4},{32,20},{48,36},{64,52},{80,68},{96,84},{112,100},{17,5},{3... | collective-permute-start | bytes 393224 | tf_op jit(solution)/shard_map/ppermute | solution.py:470
  511.5 8.6 %collective-permute-start.63 = (bf16[2,32,1024]{2,1,0:T(8,128)(2,1)S(1)}, bf16[2,32,1024]{2,1,0:T(8,128)(2,1)S(1)}, u32[]{:S(2)}, u32[]{:S(2)}) collective-permute-start(bf16[2,32,1024]{2,1,0:T(8,128)(2,1)S(1)} %get-tuple-element.365), channel_id=1, source_target_pairs={{16,8},{32,24},{48,40},{64,56},{80,72},{96,88},{112,104},{17,9},{3... | collective-permute-start | bytes 393224 | tf_op jit(solution)/shard_map/ppermute | solution.py:470
  (13 other events, 47.2 us)
